TPU v7x, 32 devices: a whole 2x2x4 slice. The times are simulated.
32 devices in a mesh: dp: 8 (over z, y), ep: 4 (over x, core).
Axes of the slice: x: 2, y: 2, z: 4, core: 2. Of those that a mesh axis runs over, the one named last changes fastest.
Arguments:
- tokens: bfloat16 [128, 4096], P(('dp', 'ep')), may hold values from -6 to 6
- router: float32 [4096, 8], replicated, may hold values from -0.1875 to 0.1875
- expert_ids: int32 [128, 2], P(('dp', 'ep')), may hold values from 0 to 7, all different within a row; in each aligned block of 4 rows (0 to 3, 4 to 7, ...) at most 2 rows name the same one
- w_gate: bfloat16 [8, 4096, 12288], P('dp', None, 'ep'), may hold values from -0.09375 to 0.09375
- w_up: bfloat16 [8, 4096, 12288], P('dp', None, 'ep'), may hold values from -0.09375 to 0.09375
- w_down: bfloat16 [8, 12288, 4096], P('dp', 'ep'), may hold values from -0.0546875 to 0.0546875
- states: bfloat16 [128, 16, 8192], P('dp', None, 'ep'), may hold values from -6 to 6
- kv_blocks: bfloat16 [256, 2, 16, 1024], P('dp', None, None, 'ep'), may hold values from -6 to 6
- plan_slots: int32 [8, 2, 3], replicated, may hold values from -1 to 15, as said below
- plan_len: int32 [8, 2], replicated, may hold values from 0 to 32, as said below
- plan_blocks: int32 [8, 2, 2, 2], replicated, may hold values from -1 to 31, as said below
Outputs:
- mixed: bfloat16 [128, 4096], P(('dp', 'ep'))
- new_states: bfloat16 [128, 16, 8192], P('dp', None, 'ep')
- new_cache: bfloat16 [256, 2, 16, 1024], P('dp', None, None, 'ep')
Inputs may be any that keep to these rules, and one draw needn't show every extreme that they name: `expert_ids`: in the rows of one device no expert is named more than 2 times. `plan_slots`: A move is live exactly where its first entry is not -1, and then all three entries are set; otherwise all are -1. For each m there is one distance d_m from 1 to 7, distinct for distinct m, such that every live move (r, m) goes to rank (r + d_m) mod 8. The leaving slots of a rank are distinct, the slots taken at a rank are distinct and differ from its leaving slots. Some rank has all 2 moves live. `plan_len`: zero exactly where the move is not live; some move holds 32 tokens. `plan_blocks`: entry j of both tables is -1 exactly where j * 16 >= plan_len. The blocks leaving a rank are distinct, the blocks taken at a rank are distinct and differ from the ones leaving it.
All inputs are finite; a program needn't handle non-finite values.
Results may differ from a plain program's by a relative error of at most 0.005.
Values may be sent and summed in bfloat16 or wider, within the bound.
A program may use at most 128 MiB of HBM per device.

v0:
```python
import functools

import jax
import jax.numpy as jnp
from jax import lax
from jax.experimental import pallas as pl
from jax.experimental.pallas import tpu as pltpu
from jax.sharding import PartitionSpec as P

CAP = 2
MESH = pl.DeviceIdType.MESH
ANY = pl.BlockSpec(memory_space=pl.ANY)
VMEM = pl.BlockSpec(memory_space=pltpu.VMEM)
SMEM = pl.BlockSpec(memory_space=pltpu.SMEM)
VMEM_LIMIT = 67_000_000
UP_TILE = 256
DOWN_TILE = 512
RING = 8


def target_rows(ids_ref, tok_count):
    picks = [ids_ref[k, t] for t in range(tok_count) for k in range(2)]
    rows = []
    for p, expert in enumerate(picks):
        slot = jnp.int32(0)
        for q in range(p):
            slot = slot + jnp.where(picks[q] == expert, 1, 0)
        rows.append(expert * CAP + slot)
    return picks, rows


def land_kernel(
    slots_ref, blocks_ref, got_state, got_cache, states_ref, kv_ref, part_ref,
    new_states, new_cache, mixed_ref, s_all, c_all, m_all, s_buf, c_buf,
    in_sem, in_s, in_c, out_sem,
):
    here = lax.axis_index("dp")
    moves, ranks = slots_ref.shape[1:]
    per_request = blocks_ref.shape[2]
    whole = ((states_ref, s_all, new_states), (kv_ref, c_all, new_cache), (part_ref, m_all, mixed_ref))
    loads = [pltpu.make_async_copy(a, b, in_sem.at[i]) for i, (a, b, _) in enumerate(whole)]
    stores = [pltpu.make_async_copy(b, c, out_sem.at[i]) for i, (_, b, c) in enumerate(whole)]
    for copy in loads:
        copy.start()
    plan = []
    for m in range(moves):
        anchor, arriving = jnp.int32(0), jnp.int32(0)
        for r in range(ranks):
            hit = slots_ref[1, m, r] == here
            anchor = jnp.where(hit, r, anchor)
            arriving = jnp.where(hit, 1, arriving)
        plan.append((anchor, arriving > 0))

    def state_load(m, anchor):
        return pltpu.make_async_copy(got_state.at[anchor], s_buf.at[m], in_s.at[m])

    def cache_load(m, j, anchor):
        return pltpu.make_async_copy(got_cache.at[anchor, j], c_buf.at[m, j], in_c.at[m, j])

    for m, (anchor, arriving) in enumerate(plan):

        @pl.when(arriving)
        def _():
            state_load(m, anchor).start()
            for j in range(per_request):
                cache_load(m, j, anchor).start()

    for copy in loads:
        copy.wait()
    stores[2].start()
    for m, (anchor, arriving) in enumerate(plan):
        slot = slots_ref[0, m, here]

        @pl.when(slot >= 0)
        def _():
            s_all[slot] = jnp.zeros_like(s_buf[m])

        for j in range(per_request):
            block = blocks_ref[m, 0, j, here]

            @pl.when(block >= 0)
            def _():
                c_all[block] = jnp.zeros_like(c_buf[m, j])

        @pl.when(arriving)
        def _():
            state_load(m, anchor).wait()
            s_all[slots_ref[2, m, anchor]] = s_buf[m]
            for j in range(per_request):
                cache_load(m, j, anchor).wait()
                spot = blocks_ref[m, 1, j, anchor]

                @pl.when(spot >= 0)
                def _():
                    c_all[spot] = c_buf[m, j]

    stores[0].start()
    stores[1].start()
    for copy in stores:
        copy.wait()


def expert_kernel(
    ranks, quads,
    ids_ref, slots_ref, len_ref, blocks_ref, tok_ref, router_ref, gate_ref, up_ref, down_ref,
    states_ref, kv_ref,
    mixed_ref, got_state, got_cache,
    packed_ref, s_all, c_all, s_pay, c_pay, send_state, send_cache, mig_load,
    g_buf, u_buf, d_buf, x_in, x_all, hidden, send_buf, recv_buf,
    g_sem, u_sem, d_sem, own_sem, first_send, first_recv, second_send, second_recv,
    back_send, back_recv, mig_send, mig_recv,
):
    d = lax.axis_index("dp")
    e = lax.axis_index("ep")
    devices = ranks * quads
    me = d * quads + e
    up_tiles = gate_ref.shape[2] // UP_TILE
    down_tiles = down_ref.shape[2] // DOWN_TILE
    ring = g_buf.shape[0]
    experts = ranks

    def up_copies(j, slot):
        columns = pl.ds(pl.multiple_of(j * UP_TILE, UP_TILE), UP_TILE)
        return (
            pltpu.make_async_copy(gate_ref.at[0, :, columns], g_buf.at[slot], g_sem.at[slot]),
            pltpu.make_async_copy(up_ref.at[0, :, columns], u_buf.at[slot], u_sem.at[slot]),
        )

    def down_copy(c):
        columns = pl.ds(pl.multiple_of(c * DOWN_TILE, DOWN_TILE), DOWN_TILE)
        return pltpu.make_async_copy(down_ref.at[0, :, columns], d_buf.at[c], d_sem.at[c])

    load_states = pltpu.make_async_copy(states_ref, s_all, mig_load.at[0])
    load_cache = pltpu.make_async_copy(kv_ref, c_all, mig_load.at[1])
    load_states.start()
    load_cache.start()
    for j in range(ring):
        for copy in up_copies(j, j):
            copy.start()

    for c in range(down_tiles):
        down_copy(c).start()

    barrier = pltpu.get_barrier_semaphore()

    @pl.loop(1, devices)
    def _(k):
        other = lax.rem(me + k, devices)
        pl.semaphore_signal(
            barrier, inc=1, device_id=(other // quads, lax.rem(other, quads)), device_id_type=MESH
        )

    tok_count = tok_ref.shape[0]
    picks, rows = target_rows(ids_ref, tok_count)
    row_at = lax.broadcasted_iota(jnp.int32, (experts * CAP, tok_count), 0)
    tok_at = lax.broadcasted_iota(jnp.int32, (experts * CAP, tok_count), 1)
    placer = jnp.zeros((experts * CAP, tok_count), jnp.float32)
    for p, row in enumerate(rows):
        placer = jnp.where((row_at == row) & (tok_at == p // 2), 1.0, placer)
    packed = jnp.dot(
        placer.astype(jnp.bfloat16), tok_ref[...], preferred_element_type=jnp.float32
    ).astype(jnp.bfloat16)
    for r in range(experts):
        packed_ref[r] = packed[r * CAP : (r + 1) * CAP]

    pl.semaphore_wait(barrier, devices - 1)

    own = pltpu.make_async_copy(packed_ref.at[d], x_in.at[me], own_sem)
    own.start()
    for k in range(1, ranks):
        peer = lax.rem(d + k, ranks)
        pltpu.make_async_remote_copy(
            packed_ref.at[peer], x_in.at[me], first_send, first_recv.at[k],
            device_id=(peer, e), device_id_type=MESH,
        ).start()

    def forward(src, slot):
        for k in range(1, quads):
            pltpu.make_async_remote_copy(
                src, x_in.at[slot], second_send, second_recv,
                device_id=(d, lax.rem(e + k, quads)), device_id_type=MESH,
            ).start()

    forward(packed_ref.at[d], me)

    wide = tok_ref[...].astype(jnp.float32)
    lane = lax.broadcasted_iota(jnp.int32, (tok_count, experts), 1)
    seat = lax.broadcasted_iota(jnp.int32, (tok_count, experts), 0)
    logits = jnp.zeros((tok_count, experts), jnp.float32)
    for r in range(experts):
        product = jnp.sum(wide * router_ref[r : r + 1, :], axis=1, keepdims=True)
        logits = jnp.where(lane == r, product, logits)
    column = lax.broadcasted_iota(jnp.int32, (tok_count, devices * CAP), 1)
    token = lax.broadcasted_iota(jnp.int32, (tok_count, devices * CAP), 0)
    row_of = (column // (quads * CAP)) * CAP + lax.rem(column, CAP)
    scores, hits = [], []
    for k in range(2):
        chosen = jnp.zeros(logits.shape, jnp.int32)
        target = jnp.zeros(column.shape, jnp.int32)
        for t in range(tok_count):
            chosen = jnp.where(seat == t, picks[2 * t + k], chosen)
            target = jnp.where(token == t, rows[2 * t + k], target)
        value = jnp.sum(jnp.where(lane == chosen, logits, 0.0), axis=1, keepdims=True)
        scores.append(jax.nn.sigmoid(value))
        hits.append(row_of == target)
    total = scores[0] + scores[1]
    comb = jnp.where(hits[0], scores[0] / total, 0.0) + jnp.where(hits[1], scores[1] / total, 0.0)
    comb_high = comb.astype(jnp.bfloat16)
    comb_low = (comb - comb_high.astype(jnp.float32)).astype(jnp.bfloat16)

    for k in range(1, ranks):
        source = lax.rem(d - k + ranks, ranks)
        slot = source * quads + e
        pltpu.make_async_remote_copy(
            x_in.at[slot], x_in.at[slot], first_send, first_recv.at[k],
            device_id=(source, e), device_id_type=MESH,
        ).wait_recv()
        forward(x_in.at[slot], slot)

    load_states.wait()
    load_cache.wait()
    moves = slots_ref.shape[1]
    per_request = blocks_ref.shape[2]
    block_len = kv_ref.shape[2]
    position = lax.broadcasted_iota(jnp.int32, kv_ref.shape[1:], 1)
    for m in range(moves):
        slot = slots_ref[0, m, d]
        s_pay[m] = jnp.zeros_like(s_pay[m])

        @pl.loop(0, s_all.shape[0])
        def _(s):
            s_pay[m] = lax.select(slot == s, s_all[s], s_pay[m])

        for j in range(per_request):
            block = blocks_ref[m, 0, j, d]
            c_pay[m, j] = jnp.zeros_like(c_pay[m, j])

            @pl.loop(0, c_all.shape[0])
            def _(s):
                c_pay[m, j] = lax.select(block == s, c_all[s], c_pay[m, j])

            kept = c_pay[m, j].astype(jnp.float32)
            kept = jnp.where(j * block_len + position < len_ref[m, d], kept, 0.0)
            c_pay[m, j] = kept.astype(jnp.bfloat16)
    for r in range(ranks):
        s_value, c_value = s_pay[0], c_pay[0]
        for m in range(1, moves):
            hit = slots_ref[1, m, d] == r
            s_value = lax.select(hit, s_pay[m], s_value)
            c_value = lax.select(hit, c_pay[m], c_value)
        send_state[r] = s_value
        send_cache[r] = c_value

    own.wait()
    arrivals = ranks * (quads - 1)
    pltpu.make_async_copy(
        x_in.at[pl.ds(0, arrivals)], x_in.at[pl.ds(0, arrivals)], second_recv
    ).wait()
    for o in range(devices):
        x_all[o * CAP : (o + 1) * CAP, :] = x_in[o]

    for k in range(1, ranks):
        peer = lax.rem(d + k, ranks)
        for i, (src, dst) in enumerate(((send_state, got_state), (send_cache, got_cache))):
            pltpu.make_async_remote_copy(
                src.at[peer], dst.at[d], mig_send.at[i], mig_recv.at[i],
                device_id=(peer, e), device_id_type=MESH,
            ).start()

    @pl.loop(0, up_tiles)
    def _(j):
        slot = lax.rem(j, ring)
        for copy in up_copies(j, slot):
            copy.wait()
        gate = jnp.dot(x_all[...], g_buf[slot], preferred_element_type=jnp.float32)
        upper = jnp.dot(x_all[...], u_buf[slot], preferred_element_type=jnp.float32)
        value = gate / (1.0 + jnp.exp(-gate)) * upper
        hidden[:, pl.ds(pl.multiple_of(j * UP_TILE, UP_TILE), UP_TILE)] = value.astype(jnp.bfloat16)

        @pl.when(j < up_tiles - ring)
        def _():
            for copy in up_copies(j + ring, slot):
                copy.start()

    @pl.loop(0, down_tiles)
    def _(c):
        down_copy(c).wait()
        part = jnp.dot(hidden[...], d_buf[c], preferred_element_type=jnp.float32)
        for o in range(devices):
            send_buf[c, o] = part[o * CAP : (o + 1) * CAP].astype(jnp.bfloat16)
        recv_buf[c, me] = send_buf[c, me]

        @pl.loop(1, devices)
        def _(k):
            other = lax.rem(me + k, devices)
            pltpu.make_async_remote_copy(
                send_buf.at[c, other], recv_buf.at[c, me], back_send.at[c], back_recv.at[c],
                device_id=(other // quads, lax.rem(other, quads)), device_id_type=MESH,
            ).start()

    @pl.loop(0, down_tiles)
    def _(c):
        most = recv_buf.at[c, pl.ds(0, devices - 1)]
        pltpu.make_async_copy(most, most, back_recv.at[c]).wait()
        rows_in = jnp.concatenate([recv_buf[c, o] for o in range(devices)], axis=0)
        high = jnp.dot(comb_high, rows_in, preferred_element_type=jnp.float32)
        low = jnp.dot(comb_low, rows_in, preferred_element_type=jnp.float32)
        mixed_ref[:, pl.ds(pl.multiple_of(c * DOWN_TILE, DOWN_TILE), DOWN_TILE)] = (
            high + low
        ).astype(jnp.bfloat16)

    for i, dst in enumerate((got_state, got_cache)):
        most = dst.at[pl.ds(0, ranks - 1)]
        pltpu.make_async_copy(most, most, mig_recv.at[i]).wait()
        pltpu.make_async_copy(most, most, mig_send.at[i]).wait()
    most = x_in.at[pl.ds(0, ranks - 1)]
    pltpu.make_async_copy(most, most, first_send).wait()
    most = x_in.at[pl.ds(0, arrivals)]
    pltpu.make_async_copy(most, most, second_send).wait()

    @pl.loop(0, down_tiles)
    def _(c):
        most = send_buf.at[c, pl.ds(0, devices - 1)]
        pltpu.make_async_copy(most, most, back_send.at[c]).wait()


def fused(
    tokens, router, expert_ids, w_gate, w_up, w_down, states, kv_blocks,
    plan_slots, plan_len, plan_blocks,
):
    ranks, quads = lax.axis_size("dp"), lax.axis_size("ep")
    devices = ranks * quads
    experts = router.shape[1]
    tok_count, width = tokens.shape
    moves = plan_slots.shape[1]
    per_request = plan_blocks.shape[3]
    bf16 = jnp.bfloat16
    dma = pltpu.SemaphoreType.DMA
    like = jax.ShapeDtypeStruct
    state_one, cache_one = states.shape[1:], kv_blocks.shape[1:]
    ids = expert_ids.T
    slots = jnp.transpose(plan_slots, (2, 1, 0))
    lengths = plan_len.T
    blocks = jnp.transpose(plan_blocks, (1, 2, 3, 0))
    depth = w_gate.shape[2]
    ring = min(RING, depth // UP_TILE)
    down_tiles = width // DOWN_TILE
    mixed, got_state, got_cache = pl.pallas_call(
        functools.partial(expert_kernel, ranks, quads),
        out_shape=(
            like((tok_count, width), bf16),
            like((ranks, *state_one), bf16),
            like((ranks, per_request, *cache_one), bf16),
        ),
        in_specs=[SMEM] * 4 + [VMEM] * 2 + [ANY] * 5,
        out_specs=(VMEM, ANY, ANY),
        scratch_shapes=[
            pltpu.VMEM((experts, CAP, width), bf16),
            pltpu.VMEM(states.shape, bf16),
            pltpu.VMEM(kv_blocks.shape, bf16),
            pltpu.VMEM((moves, *state_one), bf16),
            pltpu.VMEM((moves, per_request, *cache_one), bf16),
            pltpu.VMEM((ranks, *state_one), bf16),
            pltpu.VMEM((ranks, per_request, *cache_one), bf16),
            dma((2,)),
            pltpu.VMEM((ring, width, UP_TILE), bf16),
            pltpu.VMEM((ring, width, UP_TILE), bf16),
            pltpu.VMEM((down_tiles, depth, DOWN_TILE), bf16),
            pltpu.VMEM((devices, CAP, width), bf16),
            pltpu.VMEM((devices * CAP, width), bf16),
            pltpu.VMEM((devices * CAP, depth), bf16),
            pltpu.VMEM((down_tiles, devices, CAP, DOWN_TILE), bf16),
            pltpu.VMEM((down_tiles, devices, CAP, DOWN_TILE), bf16),
            dma((ring,)), dma((ring,)), dma((down_tiles,)), dma,
            dma, dma((ranks,)), dma, dma,
            dma((down_tiles,)), dma((down_tiles,)), dma((2,)), dma((2,)),
        ],
        compiler_params=pltpu.CompilerParams(
            collective_id=0, has_side_effects=True, vmem_limit_bytes=VMEM_LIMIT
        ),
        name="expert",
    )(
        ids, slots, lengths, blocks, tokens, router.T, w_gate, w_up, w_down, states, kv_blocks
    )
    new_states, new_cache, mixed = pl.pallas_call(
        land_kernel,
        out_shape=(like(states.shape, bf16), like(kv_blocks.shape, bf16), like(mixed.shape, bf16)),
        in_specs=[SMEM, SMEM] + [ANY] * 5,
        out_specs=(ANY, ANY, ANY),
        scratch_shapes=[
            pltpu.VMEM(states.shape, bf16),
            pltpu.VMEM(kv_blocks.shape, bf16),
            pltpu.VMEM(mixed.shape, bf16),
            pltpu.VMEM((moves, *state_one), bf16),
            pltpu.VMEM((moves, per_request, *cache_one), bf16),
            dma((3,)), dma((moves,)), dma((moves, per_request)), dma((3,)),
        ],
        name="land",
    )(slots, blocks, got_state, got_cache, states, kv_blocks, mixed)
    return mixed, new_states, new_cache


def local(
    tokens,
    router,
    expert_ids,
    w_gate,
    w_up,
    w_down,
    states,
    kv_blocks,
    plan_slots,
    plan_len,
    plan_blocks,
):
    ranks = lax.axis_size("dp")
    here = lax.axis_index("dp")
    moves = plan_slots.shape[1]
    slot_count = states.shape[0]
    block_count = kv_blocks.shape[0]
    per_request = plan_blocks.shape[3]
    block_len = kv_blocks.shape[2]
    mine = lax.dynamic_index_in_dim(plan_slots, here, 0, keepdims=False)
    my_blocks = lax.dynamic_index_in_dim(plan_blocks, here, 0, keepdims=False)
    my_length = lax.dynamic_index_in_dim(plan_len, here, 0, keepdims=False)
    leaving_slot = mine[:, 0]
    leaving_block = my_blocks[:, 0, :]
    state_out = states[jnp.maximum(leaving_slot, 0)]
    state_out = jnp.where((leaving_slot >= 0)[:, None, None], state_out, jnp.zeros_like(state_out))
    cache_out = kv_blocks[jnp.maximum(leaving_block, 0)]
    position = jnp.arange(per_request)[:, None] * block_len + jnp.arange(block_len)[None, :]
    written = (leaving_block >= 0)[:, :, None] & (position[None] < my_length[:, None, None])
    cache_out = jnp.where(written[:, :, None, :, None], cache_out, jnp.zeros_like(cache_out))
    arrivals = plan_slots[:, :, 1] == here
    sender = jnp.sum(jnp.where(arrivals, jnp.arange(ranks)[:, None], 0), axis=0)
    arriving = jnp.any(arrivals, axis=0)
    peers = jnp.arange(ranks)
    match = mine[:, 1][None, :] == peers[:, None]
    which = jnp.sum(jnp.where(match, jnp.arange(moves)[None, :], 0), axis=1)
    filled = jnp.any(match, axis=1)
    send_state = jnp.where(
        filled[:, None, None], state_out[which], jnp.zeros_like(state_out[which])
    )
    send_cache = jnp.where(
        filled[:, None, None, None, None], cache_out[which], jnp.zeros_like(cache_out[which])
    )
    got_state, got_cache = (
        lax.all_to_all(send_state, "dp", split_axis=0, concat_axis=0, tiled=True),
        lax.all_to_all(send_cache, "dp", split_axis=0, concat_axis=0, tiled=True),
    )
    state_in = got_state[sender]
    cache_in = got_cache[sender]
    slot_line = jnp.arange(slot_count)
    gone = jnp.any(slot_line[:, None] == leaving_slot[None, :], axis=1)
    new_states = jnp.where(gone[:, None, None], jnp.zeros_like(states), states)
    block_line = jnp.arange(block_count)
    gone_blocks = jnp.any(block_line[:, None, None] == leaving_block[None], axis=(1, 2))
    new_cache = jnp.where(gone_blocks[:, None, None, None], jnp.zeros_like(kv_blocks), kv_blocks)
    for move_index in range(moves):
        anchor = sender[move_index]
        place = plan_slots[anchor, move_index, 2]
        landing = (slot_line == place) & arriving[move_index]
        new_states = jnp.where(landing[:, None, None], state_in[move_index][None], new_states)
        for block_index in range(per_request):
            spot = plan_blocks[anchor, move_index, 1, block_index]
            block_hit = (block_line == spot) & arriving[move_index]
            new_cache = jnp.where(
                block_hit[:, None, None, None], cache_in[move_index, block_index][None], new_cache
            )
    experts = router.shape[1]
    tok_count = tokens.shape[0]
    width = tokens.shape[1]
    group = ranks // experts
    flat_ids = expert_ids.reshape(-1)
    onehot = (flat_ids[:, None] == jnp.arange(experts)[None, :]).astype(jnp.int32)
    earlier = jnp.cumsum(onehot, axis=0) - onehot
    slot_of = jnp.sum(earlier * onehot, axis=1)
    target_row = flat_ids * CAP + slot_of
    placer = (jnp.arange(experts * CAP)[:, None] == target_row[None, :]).astype(jnp.bfloat16)
    doubled = jnp.repeat(tokens, 2, axis=0)
    packed = jnp.dot(placer, doubled, preferred_element_type=jnp.float32).astype(jnp.bfloat16)
    outgoing = jnp.repeat(packed.reshape(experts, CAP, width), group, axis=0)
    incoming = lax.all_to_all(outgoing, "dp", split_axis=0, concat_axis=0, tiled=True)
    rows_in = incoming.reshape(ranks * CAP, width)
    piece = lax.all_gather(rows_in, "ep", axis=0, tiled=True)
    gate = jnp.dot(piece, w_gate[0], preferred_element_type=jnp.float32)
    upper = jnp.dot(piece, w_up[0], preferred_element_type=jnp.float32)
    hidden = (jax.nn.silu(gate) * upper).astype(jnp.bfloat16)
    summed = lax.psum_scatter(
        jnp.dot(hidden, w_down[0], preferred_element_type=jnp.float32),
        "ep",
        scatter_dimension=0,
        tiled=True,
    )
    returned = lax.all_to_all(
        summed.reshape(ranks, CAP, width), "dp", split_axis=0, concat_axis=0, tiled=True
    )
    expert_out = jnp.sum(returned.reshape(experts, group, CAP, width), axis=1).reshape(
        experts * CAP, width
    )
    chosen = expert_out[target_row].reshape(tok_count, 2, width)
    logits = jnp.dot(tokens.astype(jnp.float32), router, precision=lax.Precision.HIGHEST)
    scores = jax.nn.sigmoid(jnp.take_along_axis(logits, expert_ids, axis=1))
    weights = scores / jnp.sum(scores, axis=1, keepdims=True)
    mixed = jnp.sum(weights[:, :, None] * chosen, axis=1).astype(jnp.bfloat16)
    return (mixed, new_states, new_cache)


def solution(mesh):
    placed = (
        P(("dp", "ep"), None),
        P(),
        P(("dp", "ep"), None),
        P("dp", None, "ep"),
        P("dp", None, "ep"),
        P("dp", "ep", None),
        P("dp", None, "ep"),
        P("dp", None, None, "ep"),
        P(),
        P(),
        P(),
    )
    def step(*args):
        one_slab = args[1].shape[1] == lax.axis_size("dp")
        return (fused if one_slab else local)(*args)

    return jax.shard_map(
        step,
        mesh=mesh,
        in_specs=placed,
        out_specs=(P(("dp", "ep"), None), P("dp", None, "ep"), P("dp", None, None, "ep")),
        check_vma=False,
    )
```

profile of v0, /device:TPU:0, one launch (start us, length us, event | category | flops | bytes accessed | tf_op | source)
XLA Modules:
  0.0 59.2 jit_solution(18275584761322940690)
XLA Ops:
  0.6 55.0 %expert.1 = (bf16[4,4096]{1,0:T(4,128)(2,1)}, bf16[8,16,2048]{2,1,0:T(8,128)(2,1)}, bf16[8,2,2,16,256]{4,3,2,1,0:T(8,128)(2,1)}) custom-call(s32[2,4]{1,0:T(2,128)} %bitcast.10, s32[3,2,8]{2,1,0:T(2,128)} %bitcast.8, s32[2,8]{1,0:T(2,128)} %bitcast.11, s32[2,2,2,8]{3,2,1,0:T(2,128)} %bitcast.6, bf16[4,4096]{1,0:T(4,128)(2,1)} %tok_ref.1, f32[8,4096]{1,0:T(8,128)} %bitcast.5, ...), custom_call_target="tpu_custom_call" | custom-call | tf_op jit(solution)/shard_map/expert/pallas_call | solution.py:348
  55.7 3.5 %land.1 = (bf16[16,16,2048]{2,1,0:T(8,128)(2,1)}, bf16[32,2,16,256]{3,2,1,0:T(8,128)(2,1)}, bf16[4,4096]{1,0:T(4,128)(2,1)}) custom-call(s32[3,2,8]{2,1,0:T(2,128)} %bitcast.9, s32[2,2,2,8]{3,2,1,0:T(2,128)} %bitcast.7, bf16[8,16,2048]{2,1,0:T(8,128)(2,1)} %get-tuple-element.9.got_state, bf16[8,2,2,16,256]{4,3,2,1,0:T(8,128)(2,1)} %get-tuple-element.10.got_cache, ...), custom_call_target="tpu_custom_call" | custom-call | tf_op jit(solution)/shard_map/land/pallas_call | solution.py:385
where the time goes:
time: 59.4 us; the launch traced here: 59.2 us
  Pallas kernels  58.5 us (98%)
  between operations  0.64 us (1%)
    pallas_call x1, Pallas kernels, fused(): pl.pallas_call(functools.partial(expert_kernel, ranks, quads), out_shape=...  55 us
    pallas_call x1, Pallas kernels, fused(): pl.pallas_call(land_kernel, out_shape=(like(states.shape, bf16), like(kv_...  3.51 us

commit v1 on v0

v1 whole, which is shorter than its diff:
```python
import functools

import jax
import jax.numpy as jnp
from jax import lax
from jax.experimental import pallas as pl
from jax.experimental.pallas import tpu as pltpu
from jax.sharding import PartitionSpec as P

CAP = 2
MESH = pl.DeviceIdType.MESH
ANY = pl.BlockSpec(memory_space=pl.ANY)
VMEM = pl.BlockSpec(memory_space=pltpu.VMEM)
SMEM = pl.BlockSpec(memory_space=pltpu.SMEM)
VMEM_LIMIT = 65_000_000
TILE = 256
RING = 13
EARLY = 2
LAND_LIMIT = 1 << 20


def target_rows(ids_ref, tok_count):
    picks = [ids_ref[k, t] for t in range(tok_count) for k in range(2)]
    rows = []
    for p, expert in enumerate(picks):
        slot = jnp.int32(0)
        for q in range(p):
            slot = slot + jnp.where(picks[q] == expert, 1, 0)
        rows.append(expert * CAP + slot)
    return picks, rows


def land_kernel(states_ref, cache_ref, mixed_ref, new_states, new_cache, new_mixed, sem):
    pairs = ((states_ref, new_states), (cache_ref, new_cache), (mixed_ref, new_mixed))
    copies = [pltpu.make_async_copy(a, b, sem.at[i]) for i, (a, b) in enumerate(pairs)]
    for copy in copies:
        copy.start()
    for copy in copies:
        copy.wait()


def expert_kernel(
    ranks, quads,
    ids_hbm, slots_hbm, len_hbm, blocks_hbm, tok_hbm, router_hbm, gate_ref, up_ref, down_ref,
    states_ref, kv_ref,
    new_states, new_cache, mixed_ref,
    ids_ref, slots_ref, len_ref, blocks_ref, tok_ref, router_ref,
    packed_ref, s_all, c_all, s_pay, c_pay, s_got, c_got,
    w_buf, x_in, x_all, hidden, keep, pair_send, pair_recv, send_buf, recv_buf,
    small_sem, big_sem, w_sem, first_send, first_recv, cross_send, cross_recv, pair_sems,
    half_send, half_recv, back_send, back_recv, mig_send, mig_recv,
):
    d = lax.axis_index("dp")
    e = lax.axis_index("ep")
    side, core = e // 2, lax.rem(e, 2)
    across, twin = (1 - side) * 2 + core, side * 2 + 1 - core
    experts = ranks
    up_tiles = gate_ref.shape[2] // TILE
    down_tiles = down_ref.shape[2] // (2 * TILE)
    depth = down_ref.shape[1]
    ring = w_buf.shape[0]
    rows_half = 2 * ranks * CAP
    owners = 2 * ranks
    me = side * ranks + d

    barrier = pltpu.get_barrier_semaphore()

    @pl.loop(1, owners)
    def _(k):
        other = lax.rem(me + k, owners)
        pl.semaphore_signal(
            barrier, inc=1, device_id=(lax.rem(other, ranks), (other // ranks) * 2 + core),
            device_id_type=MESH,
        )

    pl.semaphore_signal(barrier, inc=1, device_id=(d, twin), device_id_type=MESH)

    smalls = [
        pltpu.make_async_copy(a, b, small_sem.at[i])
        for i, (a, b) in enumerate((
            (tok_hbm, tok_ref), (ids_hbm, ids_ref), (router_hbm, router_ref),
            (slots_hbm, slots_ref), (len_hbm, len_ref), (blocks_hbm, blocks_ref),
        ))
    ]
    for copy in smalls:
        copy.start()

    def up_copies(j):
        columns = pl.ds(pl.multiple_of(j * TILE, TILE), TILE)
        return (
            pltpu.make_async_copy(gate_ref.at[0, :, columns], w_buf.at[j, 0], w_sem.at[j, 0]),
            pltpu.make_async_copy(up_ref.at[0, :, columns], w_buf.at[j, 1], w_sem.at[j, 1]),
        )

    def down_copies(c):
        slot = lax.rem(up_tiles + c, ring)
        found = []
        for h in range(2):
            columns = pl.ds(pl.multiple_of((2 * c + h) * TILE, TILE), TILE)
            found.append(pltpu.make_async_copy(
                down_ref.at[0, :, columns], w_buf.at[slot, h, pl.ds(0, depth)], w_sem.at[slot, h]
            ))
        return found

    load_states = pltpu.make_async_copy(states_ref, s_all, big_sem.at[0])
    load_cache = pltpu.make_async_copy(kv_ref, c_all, big_sem.at[1])

    @pl.loop(0, EARLY)
    def _(j):
        for copy in up_copies(j):
            copy.start()

    load_states.start()
    load_cache.start()

    @pl.loop(EARLY, up_tiles)
    def _(j):
        for copy in up_copies(j):
            copy.start()

    @pl.loop(0, ring - up_tiles)
    def _(c):
        for copy in down_copies(c):
            copy.start()

    smalls[0].wait()
    smalls[1].wait()
    tok_count = tok_ref.shape[0]
    picks, rows = target_rows(ids_ref, tok_count)
    row_at = lax.broadcasted_iota(jnp.int32, (experts * CAP, tok_count), 0)
    tok_at = lax.broadcasted_iota(jnp.int32, (experts * CAP, tok_count), 1)
    placer = jnp.zeros((experts * CAP, tok_count), jnp.float32)
    for p, row in enumerate(rows):
        placer = jnp.where((row_at == row) & (tok_at == p // 2), 1.0, placer)
    packed = jnp.dot(
        placer.astype(jnp.bfloat16), tok_ref[...], preferred_element_type=jnp.float32
    ).astype(jnp.bfloat16)
    for r in range(experts):
        packed_ref[r] = packed[r * CAP : (r + 1) * CAP]
    x_in[e, d] = packed_ref[d]

    pl.semaphore_wait(barrier, owners)

    for k in range(1, ranks):
        peer = lax.rem(d + k, ranks)
        pltpu.make_async_remote_copy(
            packed_ref.at[peer], x_in.at[e, d], first_send, first_recv.at[k],
            device_id=(peer, e), device_id_type=MESH,
        ).start()

    def cross(src, source, k):
        return pltpu.make_async_remote_copy(
            src, x_in.at[e, source], cross_send, cross_recv.at[k],
            device_id=(d, across), device_id_type=MESH,
        )

    def to_twin(src, quad, source):
        return pltpu.make_async_remote_copy(
            src, x_in.at[quad, source], pair_sems.at[0], pair_sems.at[1],
            device_id=(d, twin), device_id_type=MESH,
        )

    cross(packed_ref.at[d], d, 0).start()
    to_twin(packed_ref.at[d], e, d).start()

    smalls[2].wait()
    wide = tok_ref[...].astype(jnp.float32)
    lane = lax.broadcasted_iota(jnp.int32, (tok_count, experts), 1)
    seat = lax.broadcasted_iota(jnp.int32, (tok_count, experts), 0)
    logits = jnp.zeros((tok_count, experts), jnp.float32)
    for r in range(experts):
        product = jnp.sum(wide * router_ref[r : r + 1, :], axis=1, keepdims=True)
        logits = jnp.where(lane == r, product, logits)
    column = lax.broadcasted_iota(jnp.int32, (tok_count, owners * CAP), 1)
    token = lax.broadcasted_iota(jnp.int32, (tok_count, owners * CAP), 0)
    row_of = lax.rem(column, ranks * CAP)
    scores, hits = [], []
    for k in range(2):
        chosen = jnp.zeros(logits.shape, jnp.int32)
        target = jnp.zeros(column.shape, jnp.int32)
        for t in range(tok_count):
            chosen = jnp.where(seat == t, picks[2 * t + k], chosen)
            target = jnp.where(token == t, rows[2 * t + k], target)
        value = jnp.sum(jnp.where(lane == chosen, logits, 0.0), axis=1, keepdims=True)
        scores.append(jax.nn.sigmoid(value))
        hits.append(row_of == target)
    total = scores[0] + scores[1]
    comb = jnp.where(hits[0], scores[0] / total, 0.0) + jnp.where(hits[1], scores[1] / total, 0.0)
    comb_high = comb.astype(jnp.bfloat16)
    comb_low = (comb - comb_high.astype(jnp.float32)).astype(jnp.bfloat16)

    def source_of(k):
        return lax.rem(d - k + ranks, ranks)

    def relay(k):
        source = source_of(k)
        cross(x_in.at[across, source], source, k).wait_recv()
        to_twin(x_in.at[across, source], across, source).start()

    for k in range(1, ranks):
        source = source_of(k)
        pltpu.make_async_remote_copy(
            packed_ref.at[d], x_in.at[e, source], first_send, first_recv.at[k],
            device_id=(source, e), device_id_type=MESH,
        ).wait_recv()
        cross(x_in.at[e, source], source, k).start()
        to_twin(x_in.at[e, source], e, source).start()
        if k >= 2:
            relay(k - 2)

    relay(ranks - 2)
    relay(ranks - 1)

    for copy in smalls[3:]:
        copy.wait()
    load_states.wait()
    load_cache.wait()
    moves = slots_ref.shape[1]
    per_request = blocks_ref.shape[2]
    block_len = kv_ref.shape[2]
    position = lax.broadcasted_iota(jnp.int32, kv_ref.shape[1:], 1)
    for m in range(moves):
        s_pay[0, m] = s_all[jnp.maximum(slots_ref[0, m, d], 0)]
        for j in range(per_request):
            kept = c_all[jnp.maximum(blocks_ref[m, 0, j, d], 0)].astype(jnp.float32)
            kept = jnp.where(j * block_len + position < len_ref[m, d], kept, 0.0)
            c_pay[0, m, j] = kept.astype(jnp.bfloat16)
    shifts = []
    for m in range(moves):
        shift = jnp.int32(0)
        for r in range(ranks):
            gap = slots_ref[1, m, r] - r
            gap = gap + jnp.where(gap < 0, ranks, 0)
            shift = jnp.where(slots_ref[1, m, r] >= 0, gap, shift)
        shifts.append(shift)
    bits = ranks.bit_length() - 1

    def bit_of(m, step):
        return 0 if step == bits - 1 else bits - 1 - (step + m) % (bits - 1)

    def hop_copies(m, step):
        bit = 1 << bit_of(m, step)
        peer = d + bit - 2 * bit * lax.rem(d // bit, 2)
        return [
            pltpu.make_async_remote_copy(
                pay.at[step, m], got.at[step, m], mig_send.at[i, step, m], mig_recv.at[i, step, m],
                device_id=(peer, e), device_id_type=MESH,
            )
            for i, (pay, got) in enumerate(((s_pay, s_got), (c_pay, c_got)))
        ]

    def hop_start(step):
        for m in range(moves):
            for copy in hop_copies(m, step):
                copy.start()

    def hop_finish(step):
        for m in range(moves):
            for copy in hop_copies(m, step):
                copy.wait_recv()
            bit = 1 << bit_of(m, step)
            fixed = sum(1 << bit_of(m, s) for s in range(step + 1))
            loose = ranks - 1 - fixed
            swap = jnp.int32(0)
            for r in range(ranks):
                reach = (r + shifts[m]) & (ranks - 1)
                held = (((d ^ r) & loose) | ((d ^ reach) & fixed)) == 0
                swap = jnp.where(held & (((d ^ r) & bit) != 0), 1, swap)
            swap = swap > 0
            s_pay[step + 1, m] = lax.select(swap, s_got[step, m], s_pay[step, m])
            c_pay[step + 1, m] = lax.select(swap, c_got[step, m], c_pay[step, m])

    hop_start(0)

    def gather(which):
        for half in range(2):
            at = pl.multiple_of((which * 2 + half) * ranks * CAP, ranks * CAP)
            x_all[pl.ds(at, ranks * CAP), :] = jnp.concatenate(
                [x_in[half * 2 + which, r] for r in range(ranks)], axis=0
            )

    gather(core)
    arrivals = x_in.at[pl.ds(0, 2)]
    pltpu.make_async_copy(arrivals, arrivals, pair_sems.at[1]).wait()
    gather(1 - core)

    def up_step(j):
        for copy in up_copies(j):
            copy.wait()
        gate = jnp.dot(x_all[...], w_buf[j, 0], preferred_element_type=jnp.float32)
        upper = jnp.dot(x_all[...], w_buf[j, 1], preferred_element_type=jnp.float32)
        value = gate / (1.0 + jnp.exp(-gate)) * upper
        hidden[:, pl.ds(pl.multiple_of(j * TILE, TILE), TILE)] = value.astype(jnp.bfloat16)
        later = j + ring - up_tiles

        @pl.when(later < down_tiles)
        def _():
            for copy in down_copies(later):
                copy.start()

    for part in range(2):
        pl.loop(part * up_tiles // 2, (part + 1) * up_tiles // 2)(up_step)
        if part + 1 < bits:
            hop_finish(part)
            hop_start(part + 1)

    def swap_copy(c):
        return pltpu.make_async_remote_copy(
            pair_send.at[c], pair_recv.at[c], half_send.at[c], half_recv.at[c],
            device_id=(d, twin), device_id_type=MESH,
        )

    def send_home(c):
        swap_copy(c).wait_recv()
        whole = (keep[c] + pair_recv[c]).astype(jnp.bfloat16)
        for o in range(owners):
            send_buf[c, o] = whole[o * CAP : (o + 1) * CAP]
        recv_buf[c, me] = send_buf[c, me]

        @pl.loop(1, owners)
        def _(k):
            other = lax.rem(me + k, owners)
            pltpu.make_async_remote_copy(
                send_buf.at[c, other], recv_buf.at[c, me], back_send.at[c], back_recv.at[c],
                device_id=(lax.rem(other, ranks), (other // ranks) * 2 + core), device_id_type=MESH,
            ).start()

    @pl.loop(0, down_tiles)
    def _(c):
        slot = lax.rem(up_tiles + c, ring)
        for copy in down_copies(c):
            copy.wait()
        for h in range(2):
            part = jnp.dot(
                hidden[...], w_buf[slot, h, pl.ds(0, depth)], preferred_element_type=jnp.float32
            )
            low, high = part[:rows_half], part[rows_half:]
            first = core == 0
            columns = pl.ds(h * TILE, TILE)
            keep[c, :, columns] = lax.select(first, low, high)
            pair_send[c, :, columns] = lax.select(first, high, low)
        swap_copy(c).start()

        @pl.when(c > 0)
        def _():
            send_home(c - 1)

    send_home(down_tiles - 1)
    hop_finish(bits - 1)

    leaving, landing = [], []
    for m in range(moves):
        anchor, arriving = jnp.int32(0), jnp.int32(0)
        for r in range(ranks):
            hit = slots_ref[1, m, r] == d
            anchor = jnp.where(hit, r, anchor)
            arriving = jnp.where(hit, 1, arriving)
        leaving.append((slots_ref[0, m, d], [blocks_ref[m, 0, j, d] for j in range(per_request)]))
        landing.append((
            jnp.where(arriving > 0, slots_ref[2, m, anchor], -1),
            [jnp.where(arriving > 0, blocks_ref[m, 1, j, anchor], -1) for j in range(per_request)],
        ))

    @pl.loop(0, s_all.shape[0])
    def _(s):
        value = s_all[s]
        for m in range(moves):
            value = lax.select(leaving[m][0] == s, jnp.zeros_like(value), value)
        for m in range(moves):
            value = lax.select(landing[m][0] == s, s_pay[bits, m], value)
        new_states[s] = value

    @pl.loop(0, c_all.shape[0])
    def _(s):
        value = c_all[s]
        for m in range(moves):
            for j in range(per_request):
                value = lax.select(leaving[m][1][j] == s, jnp.zeros_like(value), value)
        for m in range(moves):
            for j in range(per_request):
                value = lax.select(landing[m][1][j] == s, c_pay[bits, m, j], value)
        new_cache[s] = value

    @pl.loop(0, down_tiles)
    def _(c):
        most = recv_buf.at[c, pl.ds(0, owners - 1)]
        pltpu.make_async_copy(most, most, back_recv.at[c]).wait()
        rows_in = jnp.concatenate([recv_buf[c, o] for o in range(owners)], axis=0)
        high = jnp.dot(comb_high, rows_in, preferred_element_type=jnp.float32)
        low = jnp.dot(comb_low, rows_in, preferred_element_type=jnp.float32)
        mixed_ref[:, pl.ds(pl.multiple_of(c * 2 * TILE, 2 * TILE), 2 * TILE)] = (
            high + low
        ).astype(jnp.bfloat16)

    for step in range(bits):
        for m in range(moves):
            for copy in hop_copies(m, step):
                copy.wait_send()
    most = packed_ref.at[pl.ds(0, ranks - 1)]
    pltpu.make_async_copy(most, most, first_send).wait()
    most = x_in.at[0]
    pltpu.make_async_copy(most, most, cross_send).wait()
    pltpu.make_async_copy(arrivals, arrivals, pair_sems.at[0]).wait()

    @pl.loop(0, down_tiles)
    def _(c):
        swap_copy(c).wait_send()
        most = send_buf.at[c, pl.ds(0, owners - 1)]
        pltpu.make_async_copy(most, most, back_send.at[c]).wait()


def fused(
    tokens, router, expert_ids, w_gate, w_up, w_down, states, kv_blocks,
    plan_slots, plan_len, plan_blocks,
):
    ranks, quads = lax.axis_size("dp"), lax.axis_size("ep")
    experts = router.shape[1]
    tok_count, width = tokens.shape
    moves = plan_slots.shape[1]
    per_request = plan_blocks.shape[3]
    bf16 = jnp.bfloat16
    dma = pltpu.SemaphoreType.DMA
    like = jax.ShapeDtypeStruct
    state_one, cache_one = states.shape[1:], kv_blocks.shape[1:]
    ids = expert_ids.T
    slots = jnp.transpose(plan_slots, (2, 1, 0))
    lengths = plan_len.T
    blocks = jnp.transpose(plan_blocks, (1, 2, 3, 0))
    routes = router.T
    depth = w_gate.shape[2]
    down_tiles = width // (2 * TILE)
    owners = 2 * ranks
    bits = ranks.bit_length() - 1
    outputs = pl.pallas_call(
        functools.partial(expert_kernel, ranks, quads),
        out_shape=(
            pltpu.VMEM(states.shape, bf16),
            pltpu.VMEM(kv_blocks.shape, bf16),
            pltpu.VMEM(tokens.shape, bf16),
        ),
        in_specs=[ANY] * 11,
        out_specs=(VMEM, VMEM, VMEM),
        scratch_shapes=[
            pltpu.SMEM(ids.shape, jnp.int32),
            pltpu.SMEM(slots.shape, jnp.int32),
            pltpu.SMEM(lengths.shape, jnp.int32),
            pltpu.SMEM(blocks.shape, jnp.int32),
            pltpu.VMEM(tokens.shape, bf16),
            pltpu.VMEM(routes.shape, jnp.float32),
            pltpu.VMEM((experts, CAP, width), bf16),
            pltpu.VMEM(states.shape, bf16),
            pltpu.VMEM(kv_blocks.shape, bf16),
            pltpu.VMEM((bits + 1, moves, *state_one), bf16),
            pltpu.VMEM((bits + 1, moves, per_request, *cache_one), bf16),
            pltpu.VMEM((bits, moves, *state_one), bf16),
            pltpu.VMEM((bits, moves, per_request, *cache_one), bf16),
            pltpu.VMEM((RING, 2, width, TILE), bf16),
            pltpu.VMEM((quads, ranks, CAP, width), bf16),
            pltpu.VMEM((quads * ranks * CAP, width), bf16),
            pltpu.VMEM((quads * ranks * CAP, depth), bf16),
            pltpu.VMEM((down_tiles, owners * CAP, 2 * TILE), jnp.float32),
            pltpu.VMEM((down_tiles, owners * CAP, 2 * TILE), jnp.float32),
            pltpu.VMEM((down_tiles, owners * CAP, 2 * TILE), jnp.float32),
            pltpu.VMEM((down_tiles, owners, CAP, 2 * TILE), bf16),
            pltpu.VMEM((down_tiles, owners, CAP, 2 * TILE), bf16),
            dma((6,)), dma((2,)), dma((RING, 2)), dma, dma((ranks,)), dma, dma((ranks,)), dma((2,)),
            dma((down_tiles,)), dma((down_tiles,)), dma((down_tiles,)), dma((down_tiles,)),
            dma((2, bits, moves)), dma((2, bits, moves)),
        ],
        compiler_params=pltpu.CompilerParams(
            collective_id=0, has_side_effects=True, vmem_limit_bytes=VMEM_LIMIT
        ),
        name="expert",
    )(
        ids, slots, lengths, blocks, tokens, routes, w_gate, w_up, w_down, states, kv_blocks
    )
    outputs = [pltpu.with_memory_space_constraint(o, pltpu.VMEM) for o in outputs]
    new_states, new_cache, mixed = pl.pallas_call(
        land_kernel,
        out_shape=(like(states.shape, bf16), like(kv_blocks.shape, bf16), like(tokens.shape, bf16)),
        in_specs=[VMEM] * 3,
        out_specs=(ANY, ANY, ANY),
        scratch_shapes=[dma((3,))],
        compiler_params=pltpu.CompilerParams(vmem_limit_bytes=LAND_LIMIT),
        name="land",
    )(*outputs)
    return mixed, new_states, new_cache


def local(
    tokens,
    router,
    expert_ids,
    w_gate,
    w_up,
    w_down,
    states,
    kv_blocks,
    plan_slots,
    plan_len,
    plan_blocks,
):
    ranks = lax.axis_size("dp")
    here = lax.axis_index("dp")
    moves = plan_slots.shape[1]
    slot_count = states.shape[0]
    block_count = kv_blocks.shape[0]
    per_request = plan_blocks.shape[3]
    block_len = kv_blocks.shape[2]
    mine = lax.dynamic_index_in_dim(plan_slots, here, 0, keepdims=False)
    my_blocks = lax.dynamic_index_in_dim(plan_blocks, here, 0, keepdims=False)
    my_length = lax.dynamic_index_in_dim(plan_len, here, 0, keepdims=False)
    leaving_slot = mine[:, 0]
    leaving_block = my_blocks[:, 0, :]
    state_out = states[jnp.maximum(leaving_slot, 0)]
    state_out = jnp.where((leaving_slot >= 0)[:, None, None], state_out, jnp.zeros_like(state_out))
    cache_out = kv_blocks[jnp.maximum(leaving_block, 0)]
    position = jnp.arange(per_request)[:, None] * block_len + jnp.arange(block_len)[None, :]
    written = (leaving_block >= 0)[:, :, None] & (position[None] < my_length[:, None, None])
    cache_out = jnp.where(written[:, :, None, :, None], cache_out, jnp.zeros_like(cache_out))
    arrivals = plan_slots[:, :, 1] == here
    sender = jnp.sum(jnp.where(arrivals, jnp.arange(ranks)[:, None], 0), axis=0)
    arriving = jnp.any(arrivals, axis=0)
    peers = jnp.arange(ranks)
    match = mine[:, 1][None, :] == peers[:, None]
    which = jnp.sum(jnp.where(match, jnp.arange(moves)[None, :], 0), axis=1)
    filled = jnp.any(match, axis=1)
    send_state = jnp.where(
        filled[:, None, None], state_out[which], jnp.zeros_like(state_out[which])
    )
    send_cache = jnp.where(
        filled[:, None, None, None, None], cache_out[which], jnp.zeros_like(cache_out[which])
    )
    got_state, got_cache = (
        lax.all_to_all(send_state, "dp", split_axis=0, concat_axis=0, tiled=True),
        lax.all_to_all(send_cache, "dp", split_axis=0, concat_axis=0, tiled=True),
    )
    state_in = got_state[sender]
    cache_in = got_cache[sender]
    slot_line = jnp.arange(slot_count)
    gone = jnp.any(slot_line[:, None] == leaving_slot[None, :], axis=1)
    new_states = jnp.where(gone[:, None, None], jnp.zeros_like(states), states)
    block_line = jnp.arange(block_count)
    gone_blocks = jnp.any(block_line[:, None, None] == leaving_block[None], axis=(1, 2))
    new_cache = jnp.where(gone_blocks[:, None, None, None], jnp.zeros_like(kv_blocks), kv_blocks)
    for move_index in range(moves):
        anchor = sender[move_index]
        place = plan_slots[anchor, move_index, 2]
        landing = (slot_line == place) & arriving[move_index]
        new_states = jnp.where(landing[:, None, None], state_in[move_index][None], new_states)
        for block_index in range(per_request):
            spot = plan_blocks[anchor, move_index, 1, block_index]
            block_hit = (block_line == spot) & arriving[move_index]
            new_cache = jnp.where(
                block_hit[:, None, None, None], cache_in[move_index, block_index][None], new_cache
            )
    experts = router.shape[1]
    tok_count = tokens.shape[0]
    width = tokens.shape[1]
    group = ranks // experts
    flat_ids = expert_ids.reshape(-1)
    onehot = (flat_ids[:, None] == jnp.arange(experts)[None, :]).astype(jnp.int32)
    earlier = jnp.cumsum(onehot, axis=0) - onehot
    slot_of = jnp.sum(earlier * onehot, axis=1)
    target_row = flat_ids * CAP + slot_of
    placer = (jnp.arange(experts * CAP)[:, None] == target_row[None, :]).astype(jnp.bfloat16)
    doubled = jnp.repeat(tokens, 2, axis=0)
    packed = jnp.dot(placer, doubled, preferred_element_type=jnp.float32).astype(jnp.bfloat16)
    outgoing = jnp.repeat(packed.reshape(experts, CAP, width), group, axis=0)
    incoming = lax.all_to_all(outgoing, "dp", split_axis=0, concat_axis=0, tiled=True)
    rows_in = incoming.reshape(ranks * CAP, width)
    piece = lax.all_gather(rows_in, "ep", axis=0, tiled=True)
    gate = jnp.dot(piece, w_gate[0], preferred_element_type=jnp.float32)
    upper = jnp.dot(piece, w_up[0], preferred_element_type=jnp.float32)
    hidden = (jax.nn.silu(gate) * upper).astype(jnp.bfloat16)
    summed = lax.psum_scatter(
        jnp.dot(hidden, w_down[0], preferred_element_type=jnp.float32),
        "ep",
        scatter_dimension=0,
        tiled=True,
    )
    returned = lax.all_to_all(
        summed.reshape(ranks, CAP, width), "dp", split_axis=0, concat_axis=0, tiled=True
    )
    expert_out = jnp.sum(returned.reshape(experts, group, CAP, width), axis=1).reshape(
        experts * CAP, width
    )
    chosen = expert_out[target_row].reshape(tok_count, 2, width)
    logits = jnp.dot(tokens.astype(jnp.float32), router, precision=lax.Precision.HIGHEST)
    scores = jax.nn.sigmoid(jnp.take_along_axis(logits, expert_ids, axis=1))
    weights = scores / jnp.sum(scores, axis=1, keepdims=True)
    mixed = jnp.sum(weights[:, :, None] * chosen, axis=1).astype(jnp.bfloat16)
    return (mixed, new_states, new_cache)


def solution(mesh):
    placed = (
        P(("dp", "ep"), None),
        P(),
        P(("dp", "ep"), None),
        P("dp", None, "ep"),
        P("dp", None, "ep"),
        P("dp", "ep", None),
        P("dp", None, "ep"),
        P("dp", None, None, "ep"),
        P(),
        P(),
        P(),
    )
    def step(*args):
        ranks, quads = lax.axis_size("dp"), lax.axis_size("ep")
        one_slab = args[1].shape[1] == ranks and ranks & (ranks - 1) == 0
        two_by_two = quads == 2 * 2
        return (fused if one_slab and two_by_two else local)(*args)

    return jax.shard_map(
        step,
        mesh=mesh,
        in_specs=placed,
        out_specs=(P(("dp", "ep"), None), P("dp", None, "ep"), P("dp", None, None, "ep")),
        check_vma=False,
    )
```

time: 59.4 us -> 46.6 us (0.78)
  Pallas kernels: 58.5 us -> 45.8 us
    pallas_call x1, Pallas kernels: 55 us -> 44.6 us  [fused(): pl.pallas_call(functools.partial(expert_kernel, ranks, quads), out_shape=...]
    pallas_call x1, Pallas kernels: 3.51 us -> 1.17 us  [fused(): pl.pallas_call(land_kernel, out_shape=(like(states.shape, bf16), like(kv_...]
where the time goes in v1:
time: 46.6 us; the launch traced here: 46.4 us
  Pallas kernels  45.8 us (98%)
  between operations  0.64 us (1%)
    pallas_call x1, Pallas kernels, fused(): pl.pallas_call(functools.partial(expert_kernel, ranks, quads), out_shape=...  44.6 us
    pallas_call x1, Pallas kernels, fused(): pl.pallas_call(land_kernel, out_shape=(like(states.shape, bf16), like(kv_...  1.17 us

profile of v1, /device:TPU:0, one launch (start us, length us, event | category | flops | bytes accessed | tf_op | source)
XLA Modules:
  0.0 46.4 jit_solution(12954385770881103226)
XLA Ops:
  0.6 44.6 %expert.1 = (bf16[16,16,2048]{2,1,0:T(8,128)(2,1)S(1)}, bf16[32,2,16,256]{3,2,1,0:T(8,128)(2,1)S(1)}, bf16[4,4096]{1,0:T(4,128)(2,1)S(1)}) custom-call(s32[2,4]{1,0:T(2,128)} %bitcast.8, s32[3,2,8]{2,1,0:T(2,128)} %bitcast.7, s32[2,8]{1,0:T(2,128)} %bitcast.9, s32[2,2,2,8]{3,2,1,0:T(2,128)} %bitcast.6, bf16[4,4096]{1,0:T(4,128)(2,1)} %tok_hbm.1, ...), custom_call_target="tpu_custom_call" | custom-call | tf_op jit(solution)/shard_map/expert/pallas_call | solution.py:434
  45.3 1.2 %land.1 = (bf16[16,16,2048]{2,1,0:T(8,128)(2,1)}, bf16[32,2,16,256]{3,2,1,0:T(8,128)(2,1)}, bf16[4,4096]{1,0:T(4,128)(2,1)}) custom-call(bf16[16,16,2048]{2,1,0:T(8,128)(2,1)S(1)} %get-tuple-element.9.states_ref, bf16[32,2,16,256]{3,2,1,0:T(8,128)(2,1)S(1)} %get-tuple-element.10.cache_ref, bf16[4,4096]{1,0:T(4,128)(2,1)S(1)} %get-tuple-element.11.mixed_ref), custom_call_target="tpu_custom_call" | custom-call | tf_op jit(solution)/shard_map/land/pallas_call | solution.py:478

commit v2 on v1

--- a/solution.py
+++ b/solution.py
@@ -16,6 +16,9 @@
 TILE = 256
 RING = 13
 EARLY = 2
+WIDE = 2
+PARTS = 2
+SPLIT = 3
 LAND_LIMIT = 1 << 20
 
 
@@ -45,15 +48,16 @@
     states_ref, kv_ref,
     new_states, new_cache, mixed_ref,
     ids_ref, slots_ref, len_ref, blocks_ref, tok_ref, router_ref,
-    packed_ref, s_all, c_all, s_pay, c_pay, s_got, c_got,
-    w_buf, x_in, x_all, hidden, keep, pair_send, pair_recv, send_buf, recv_buf,
-    small_sem, big_sem, w_sem, first_send, first_recv, cross_send, cross_recv, pair_sems,
+    packed_ref, s_all, c_all, pay, got,
+    w_buf, x_in, x_all, part_sum, hidden, wide_keep, wide_pair, wide_home, slim_keep, slim_pair, slim_home,
+    small_sem, big_sem, w_sem, first_send, first_recv, cross_send, cross_recv, pair_send, pair_recv,
     half_send, half_recv, back_send, back_recv, mig_send, mig_recv,
 ):
     d = lax.axis_index("dp")
     e = lax.axis_index("ep")
     side, core = e // 2, lax.rem(e, 2)
     across, twin = (1 - side) * 2 + core, side * 2 + 1 - core
+    diagonal = (1 - side) * 2 + 1 - core
     experts = ranks
     up_tiles = gate_ref.shape[2] // TILE
     down_tiles = down_ref.shape[2] // (2 * TILE)
@@ -61,6 +65,7 @@
     ring = w_buf.shape[0]
     rows_half = 2 * ranks * CAP
     owners = 2 * ranks
+    span = packed_ref.shape[3]
     me = side * ranks + d
 
     barrier = pltpu.get_barrier_semaphore()
@@ -73,7 +78,8 @@
             device_id_type=MESH,
         )
 
-    pl.semaphore_signal(barrier, inc=1, device_id=(d, twin), device_id_type=MESH)
+    for quad in (twin, diagonal):
+        pl.semaphore_signal(barrier, inc=1, device_id=(d, quad), device_id_type=MESH)
 
     smalls = [
         pltpu.make_async_copy(a, b, small_sem.at[i])
@@ -88,9 +94,12 @@
     def up_copies(j):
         columns = pl.ds(pl.multiple_of(j * TILE, TILE), TILE)
         return (
-            pltpu.make_async_copy(gate_ref.at[0, :, columns], w_buf.at[j, 0], w_sem.at[j, 0]),
-            pltpu.make_async_copy(up_ref.at[0, :, columns], w_buf.at[j, 1], w_sem.at[j, 1]),
+            pltpu.make_async_copy(gate_ref.at[0, :, columns], w_buf.at[j, 0], w_sem.at[j]),
+            pltpu.make_async_copy(up_ref.at[0, :, columns], w_buf.at[j, 1], w_sem.at[j]),
         )
+
+    def up_wait(j):
+        pltpu.make_async_copy(w_buf.at[j], w_buf.at[j], w_sem.at[j]).wait()
 
     def down_copies(c):
         slot = lax.rem(up_tiles + c, ring)
@@ -98,9 +107,14 @@
         for h in range(2):
             columns = pl.ds(pl.multiple_of((2 * c + h) * TILE, TILE), TILE)
             found.append(pltpu.make_async_copy(
-                down_ref.at[0, :, columns], w_buf.at[slot, h, pl.ds(0, depth)], w_sem.at[slot, h]
+                down_ref.at[0, :, columns], w_buf.at[slot, h, pl.ds(0, depth)], w_sem.at[slot]
             ))
         return found
+
+    def down_wait(c):
+        slot = lax.rem(up_tiles + c, ring)
+        both = w_buf.at[slot, :, pl.ds(0, depth)]
+        pltpu.make_async_copy(both, both, w_sem.at[slot]).wait()
 
     load_states = pltpu.make_async_copy(states_ref, s_all, big_sem.at[0])
     load_cache = pltpu.make_async_copy(kv_ref, c_all, big_sem.at[1])
@@ -135,33 +149,53 @@
     packed = jnp.dot(
         placer.astype(jnp.bfloat16), tok_ref[...], preferred_element_type=jnp.float32
     ).astype(jnp.bfloat16)
-    for r in range(experts):
-        packed_ref[r] = packed[r * CAP : (r + 1) * CAP]
-    x_in[e, d] = packed_ref[d]
-
-    pl.semaphore_wait(barrier, owners)
-
-    for k in range(1, ranks):
-        peer = lax.rem(d + k, ranks)
-        pltpu.make_async_remote_copy(
-            packed_ref.at[peer], x_in.at[e, d], first_send, first_recv.at[k],
-            device_id=(peer, e), device_id_type=MESH,
-        ).start()
-
-    def cross(src, source, k):
+    for h in range(PARTS):
+        for r in range(experts):
+            packed_ref[h, r] = packed[r * CAP : (r + 1) * CAP, h * span : (h + 1) * span]
+        x_in[h, e, d] = packed_ref[h, d]
+
+    pl.semaphore_wait(barrier, owners + 1)
+
+    z_count = ranks // 2
+
+    def planes(i, reverse):
+        forward = (d // 2 < z_count // 2) == (not reverse)
+        return jnp.where(forward, i, z_count - 1 - i)
+
+    def cross(src, h, source):
         return pltpu.make_async_remote_copy(
-            src, x_in.at[e, source], cross_send, cross_recv.at[k],
+            src, x_in.at[h, e, source], cross_send, cross_recv.at[h, source],
             device_id=(d, across), device_id_type=MESH,
         )
 
-    def to_twin(src, quad, source):
+    def to_other(src, h, quad, source, where):
         return pltpu.make_async_remote_copy(
-            src, x_in.at[quad, source], pair_sems.at[0], pair_sems.at[1],
-            device_id=(d, twin), device_id_type=MESH,
+            src, x_in.at[h, quad, source], pair_send, pair_recv.at[h],
+            device_id=(d, where), device_id_type=MESH,
         )
 
-    cross(packed_ref.at[d], d, 0).start()
-    to_twin(packed_ref.at[d], e, d).start()
+    def spread(src, h, source):
+        cross(src, h, source).start()
+        to_other(src, h, e, source, twin).start()
+
+        @pl.when(core == 0)
+        def _():
+            to_other(src, h, e, source, diagonal).start()
+
+    for h in range(PARTS):
+        for i in range(z_count):
+            plane = planes(i, True)
+            for y in range(2):
+                peer = plane * 2 + y
+
+                @pl.when(peer != d)
+                def _():
+                    pltpu.make_async_remote_copy(
+                        packed_ref.at[h, peer], x_in.at[h, e, d], first_send, first_recv.at[h, d],
+                        device_id=(peer, e), device_id_type=MESH,
+                    ).start()
+
+        spread(packed_ref.at[h, d], h, d)
 
     smalls[2].wait()
     wide = tok_ref[...].astype(jnp.float32)
@@ -189,27 +223,26 @@
     comb_high = comb.astype(jnp.bfloat16)
     comb_low = (comb - comb_high.astype(jnp.float32)).astype(jnp.bfloat16)
 
-    def source_of(k):
-        return lax.rem(d - k + ranks, ranks)
-
-    def relay(k):
-        source = source_of(k)
-        cross(x_in.at[across, source], source, k).wait_recv()
-        to_twin(x_in.at[across, source], across, source).start()
-
-    for k in range(1, ranks):
-        source = source_of(k)
-        pltpu.make_async_remote_copy(
-            packed_ref.at[d], x_in.at[e, source], first_send, first_recv.at[k],
-            device_id=(source, e), device_id_type=MESH,
-        ).wait_recv()
-        cross(x_in.at[e, source], source, k).start()
-        to_twin(x_in.at[e, source], e, source).start()
-        if k >= 2:
-            relay(k - 2)
-
-    relay(ranks - 2)
-    relay(ranks - 1)
+    near = [planes(i, False) * 2 + y for i in range(z_count) for y in range(2)]
+
+    def relay(h):
+        for source in near:
+            cross(x_in.at[h, across, source], h, source).wait_recv()
+
+            @pl.when(core == 1)
+            def _():
+                to_other(x_in.at[h, across, source], h, across, source, twin).start()
+
+    for h in range(PARTS):
+        for source in near:
+
+            @pl.when(source != d)
+            def _():
+                pltpu.make_async_remote_copy(
+                    packed_ref.at[h, d], x_in.at[h, e, source], first_send, first_recv.at[h, source],
+                    device_id=(source, e), device_id_type=MESH,
+                ).wait_recv()
+                spread(x_in.at[h, e, source], h, source)
 
     for copy in smalls[3:]:
         copy.wait()
@@ -217,14 +250,17 @@
     load_cache.wait()
     moves = slots_ref.shape[1]
     per_request = blocks_ref.shape[2]
-    block_len = kv_ref.shape[2]
+    block_len, lanes = kv_ref.shape[2:]
+    pieces = states_ref.shape[2] // lanes
     position = lax.broadcasted_iota(jnp.int32, kv_ref.shape[1:], 1)
     for m in range(moves):
-        s_pay[0, m] = s_all[jnp.maximum(slots_ref[0, m, d], 0)]
+        state = s_all[jnp.maximum(slots_ref[0, m, d], 0)]
+        for i in range(pieces):
+            pay[0, m, i] = state[:, i * lanes : (i + 1) * lanes]
         for j in range(per_request):
             kept = c_all[jnp.maximum(blocks_ref[m, 0, j, d], 0)].astype(jnp.float32)
             kept = jnp.where(j * block_len + position < len_ref[m, d], kept, 0.0)
-            c_pay[0, m, j] = kept.astype(jnp.bfloat16)
+            pay[0, m, pl.ds(pieces + 2 * j, 2)] = kept.astype(jnp.bfloat16)
     shifts = []
     for m in range(moves):
         shift = jnp.int32(0)
@@ -238,26 +274,21 @@
     def bit_of(m, step):
         return 0 if step == bits - 1 else bits - 1 - (step + m) % (bits - 1)
 
-    def hop_copies(m, step):
+    def hop_copy(m, step):
         bit = 1 << bit_of(m, step)
         peer = d + bit - 2 * bit * lax.rem(d // bit, 2)
-        return [
-            pltpu.make_async_remote_copy(
-                pay.at[step, m], got.at[step, m], mig_send.at[i, step, m], mig_recv.at[i, step, m],
-                device_id=(peer, e), device_id_type=MESH,
-            )
-            for i, (pay, got) in enumerate(((s_pay, s_got), (c_pay, c_got)))
-        ]
+        return pltpu.make_async_remote_copy(
+            pay.at[step, m], got.at[step, m], mig_send, mig_recv.at[step],
+            device_id=(peer, e), device_id_type=MESH,
+        )
 
     def hop_start(step):
         for m in range(moves):
-            for copy in hop_copies(m, step):
-                copy.start()
+            hop_copy(m, step).start()
 
     def hop_finish(step):
+        pltpu.make_async_copy(got.at[step], got.at[step], mig_recv.at[step]).wait()
         for m in range(moves):
-            for copy in hop_copies(m, step):
-                copy.wait_recv()
             bit = 1 << bit_of(m, step)
             fixed = sum(1 << bit_of(m, s) for s in range(step + 1))
             loose = ranks - 1 - fixed
@@ -266,31 +297,35 @@
                 reach = (r + shifts[m]) & (ranks - 1)
                 held = (((d ^ r) & loose) | ((d ^ reach) & fixed)) == 0
                 swap = jnp.where(held & (((d ^ r) & bit) != 0), 1, swap)
-            swap = swap > 0
-            s_pay[step + 1, m] = lax.select(swap, s_got[step, m], s_pay[step, m])
-            c_pay[step + 1, m] = lax.select(swap, c_got[step, m], c_pay[step, m])
+            pay[step + 1, m] = lax.select(swap > 0, got[step, m], pay[step, m])
 
     hop_start(0)
-
-    def gather(which):
+    relay(0)
+
+    def gather(h, which):
         for half in range(2):
             at = pl.multiple_of((which * 2 + half) * ranks * CAP, ranks * CAP)
-            x_all[pl.ds(at, ranks * CAP), :] = jnp.concatenate(
-                [x_in[half * 2 + which, r] for r in range(ranks)], axis=0
+            x_all[pl.ds(at, ranks * CAP), h * span : (h + 1) * span] = jnp.concatenate(
+                [x_in[h, half * 2 + which, r] for r in range(ranks)], axis=0
             )
 
-    gather(core)
-    arrivals = x_in.at[pl.ds(0, 2)]
-    pltpu.make_async_copy(arrivals, arrivals, pair_sems.at[1]).wait()
-    gather(1 - core)
-
-    def up_step(j):
-        for copy in up_copies(j):
-            copy.wait()
-        gate = jnp.dot(x_all[...], w_buf[j, 0], preferred_element_type=jnp.float32)
-        upper = jnp.dot(x_all[...], w_buf[j, 1], preferred_element_type=jnp.float32)
+    def pair_wait(h):
+        most = x_in.at[h, pl.ds(0, 2)]
+        pltpu.make_async_copy(most, most, pair_recv.at[h]).wait()
+
+    gather(0, core)
+    pair_wait(0)
+    gather(0, 1 - core)
+
+    def product(j, which, h):
+        rows_of = pl.ds(h * span, span)
+        return jnp.dot(x_all[:, rows_of], w_buf[j, which, rows_of], preferred_element_type=jnp.float32)
+
+    def finish_up(j, gate, upper):
         value = gate / (1.0 + jnp.exp(-gate)) * upper
         hidden[:, pl.ds(pl.multiple_of(j * TILE, TILE), TILE)] = value.astype(jnp.bfloat16)
+
+    def refill(j):
         later = j + ring - up_tiles
 
         @pl.when(later < down_tiles)
@@ -298,54 +333,120 @@
             for copy in down_copies(later):
                 copy.start()
 
-    for part in range(2):
-        pl.loop(part * up_tiles // 2, (part + 1) * up_tiles // 2)(up_step)
-        if part + 1 < bits:
-            hop_finish(part)
-            hop_start(part + 1)
-
-    def swap_copy(c):
+    def tiles_of(i):
+        return [i * WIDE + n for n in range(WIDE)]
+
+    def first_step(i):
+        for j in tiles_of(i):
+            up_wait(j)
+        for j in tiles_of(i):
+            for which in range(2):
+                part_sum[j, which] = product(j, which, 0)
+
+    def second_step(i):
+        for j in tiles_of(i):
+            sums = [part_sum[j, which] for which in range(2)]
+            for h in range(1, PARTS):
+                sums = [sums[which] + product(j, which, h) for which in range(2)]
+            finish_up(j, *sums)
+        for j in tiles_of(i):
+            refill(j)
+
+    def whole_step(i):
+        for j in tiles_of(i):
+            up_wait(j)
+        for j in tiles_of(i):
+            gate, upper = [
+                jnp.dot(x_all[...], w_buf[j, which], preferred_element_type=jnp.float32)
+                for which in range(2)
+            ]
+            finish_up(j, gate, upper)
+        for j in tiles_of(i):
+            refill(j)
+
+    split = part_sum.shape[0] // WIDE
+    pl.loop(0, split - 1)(first_step)
+    for h in range(1, PARTS):
+        relay(h)
+        gather(h, core)
+    pl.loop(split - 1, split)(first_step)
+    for h in range(1, PARTS):
+        pair_wait(h)
+        gather(h, 1 - core)
+    hop_finish(0)
+    hop_start(1)
+    pl.loop(0, split)(second_step)
+    pl.loop(split, up_tiles // WIDE)(whole_step)
+    for step in range(1, bits - 1):
+        hop_finish(step)
+        hop_start(step + 1)
+
+    wide_count = wide_keep.shape[0]
+    groups = [(0, g, 2 * g, 2) for g in range(wide_count)]
+    groups += [(1, g, 2 * wide_count + g, 1) for g in range(slim_keep.shape[0])]
+    stores = ((wide_keep, wide_pair, wide_home), (slim_keep, slim_pair, slim_home))
+
+    def swap_copy(n):
+        kind, g, _, _ = groups[n]
+        pair = stores[kind][1]
         return pltpu.make_async_remote_copy(
-            pair_send.at[c], pair_recv.at[c], half_send.at[c], half_recv.at[c],
+            pair.at[0, g], pair.at[1, g], half_send, half_recv.at[n],
             device_id=(d, twin), device_id_type=MESH,
         )
 
-    def send_home(c):
-        swap_copy(c).wait_recv()
-        whole = (keep[c] + pair_recv[c]).astype(jnp.bfloat16)
+    def send_home(n):
+        kind, g, _, _ = groups[n]
+        keep, pair, home = stores[kind]
+        swap_copy(n).wait_recv()
+        whole = (keep[g] + pair[1, g]).astype(jnp.bfloat16)
         for o in range(owners):
-            send_buf[c, o] = whole[o * CAP : (o + 1) * CAP]
-        recv_buf[c, me] = send_buf[c, me]
-
-        @pl.loop(1, owners)
+            home[0, g, o] = whole[o * CAP : (o + 1) * CAP]
+        home[1, g, me] = home[0, g, me]
+
+        @pl.loop(1, owners, unroll=True)
         def _(k):
             other = lax.rem(me + k, owners)
             pltpu.make_async_remote_copy(
-                send_buf.at[c, other], recv_buf.at[c, me], back_send.at[c], back_recv.at[c],
+                home.at[0, g, other], home.at[1, g, me], back_send, back_recv.at[n],
                 device_id=(lax.rem(other, ranks), (other // ranks) * 2 + core), device_id_type=MESH,
             ).start()
 
-    @pl.loop(0, down_tiles)
-    def _(c):
-        slot = lax.rem(up_tiles + c, ring)
-        for copy in down_copies(c):
-            copy.wait()
-        for h in range(2):
-            part = jnp.dot(
-                hidden[...], w_buf[slot, h, pl.ds(0, depth)], preferred_element_type=jnp.float32
-            )
-            low, high = part[:rows_half], part[rows_half:]
-            first = core == 0
-            columns = pl.ds(h * TILE, TILE)
-            keep[c, :, columns] = lax.select(first, low, high)
-            pair_send[c, :, columns] = lax.select(first, high, low)
-        swap_copy(c).start()
-
-        @pl.when(c > 0)
-        def _():
-            send_home(c - 1)
-
-    send_home(down_tiles - 1)
+    def multiply(n):
+        kind, g, start, count = groups[n]
+        keep, pair, _ = stores[kind]
+        for c in range(start, start + count):
+            down_wait(c)
+        for c in range(start, start + count):
+            slot = lax.rem(up_tiles + c, ring)
+            for h in range(2):
+                part = jnp.dot(
+                    hidden[...], w_buf[slot, h, pl.ds(0, depth)], preferred_element_type=jnp.float32
+                )
+                low, high = part[:rows_half], part[rows_half:]
+                first = core == 0
+                columns = pl.ds((2 * (c - start) + h) * TILE, TILE)
+                keep[g, :, columns] = lax.select(first, low, high)
+                pair[0, g, :, columns] = lax.select(first, high, low)
+        swap_copy(n).start()
+
+    def mix(n):
+        kind, g, start, count = groups[n]
+        home = stores[kind][2]
+        most = home.at[1, g, pl.ds(0, owners - 1)]
+        pltpu.make_async_copy(most, most, back_recv.at[n]).wait()
+        rows_in = jnp.concatenate([home[1, g, o] for o in range(owners)], axis=0)
+        high = jnp.dot(comb_high, rows_in, preferred_element_type=jnp.float32)
+        low = jnp.dot(comb_low, rows_in, preferred_element_type=jnp.float32)
+        mixed_ref[:, start * 2 * TILE : (start + count) * 2 * TILE] = (high + low).astype(jnp.bfloat16)
+
+    for n in range(len(groups)):
+        multiply(n)
+        if n > 0:
+            send_home(n - 1)
+    send_home(len(groups) - 1)
+    early = max(len(groups) - 2, 0)
+    for n in range(early):
+        mix(n)
     hop_finish(bits - 1)
 
     leaving, landing = [], []
@@ -367,7 +468,8 @@
         for m in range(moves):
             value = lax.select(leaving[m][0] == s, jnp.zeros_like(value), value)
         for m in range(moves):
-            value = lax.select(landing[m][0] == s, s_pay[bits, m], value)
+            moved = jnp.concatenate([pay[bits, m, i] for i in range(pieces)], axis=1)
+            value = lax.select(landing[m][0] == s, moved, value)
         new_states[s] = value
 
     @pl.loop(0, c_all.shape[0])
@@ -378,35 +480,24 @@
                 value = lax.select(leaving[m][1][j] == s, jnp.zeros_like(value), value)
         for m in range(moves):
             for j in range(per_request):
-                value = lax.select(landing[m][1][j] == s, c_pay[bits, m, j], value)
+                value = lax.select(landing[m][1][j] == s, pay[bits, m, pl.ds(pieces + 2 * j, 2)], value)
         new_cache[s] = value
 
-    @pl.loop(0, down_tiles)
-    def _(c):
-        most = recv_buf.at[c, pl.ds(0, owners - 1)]
-        pltpu.make_async_copy(most, most, back_recv.at[c]).wait()
-        rows_in = jnp.concatenate([recv_buf[c, o] for o in range(owners)], axis=0)
-        high = jnp.dot(comb_high, rows_in, preferred_element_type=jnp.float32)
-        low = jnp.dot(comb_low, rows_in, preferred_element_type=jnp.float32)
-        mixed_ref[:, pl.ds(pl.multiple_of(c * 2 * TILE, 2 * TILE), 2 * TILE)] = (
-            high + low
-        ).astype(jnp.bfloat16)
+    for n in range(early, len(groups)):
+        mix(n)
 
     for step in range(bits):
-        for m in range(moves):
-            for copy in hop_copies(m, step):
-                copy.wait_send()
-    most = packed_ref.at[pl.ds(0, ranks - 1)]
+        pltpu.make_async_copy(pay.at[step], pay.at[step], mig_send).wait()
+    most = packed_ref.at[:, pl.ds(0, ranks - 1)]
     pltpu.make_async_copy(most, most, first_send).wait()
-    most = x_in.at[0]
+    most = x_in.at[:, 0]
     pltpu.make_async_copy(most, most, cross_send).wait()
-    pltpu.make_async_copy(arrivals, arrivals, pair_sems.at[0]).wait()
-
-    @pl.loop(0, down_tiles)
-    def _(c):
-        swap_copy(c).wait_send()
-        most = send_buf.at[c, pl.ds(0, owners - 1)]
-        pltpu.make_async_copy(most, most, back_send.at[c]).wait()
+    most = x_in.at[:, pl.ds(0, 2)]
+    pltpu.make_async_copy(most, most, pair_send).wait()
+    for _, pair, home in stores:
+        pltpu.make_async_copy(pair.at[0], pair.at[0], half_send).wait()
+        most = home.at[0, :, pl.ds(0, owners - 1)]
+        pltpu.make_async_copy(most, most, back_send).wait()
 
 
 def fused(
@@ -421,7 +512,6 @@
     bf16 = jnp.bfloat16
     dma = pltpu.SemaphoreType.DMA
     like = jax.ShapeDtypeStruct
-    state_one, cache_one = states.shape[1:], kv_blocks.shape[1:]
     ids = expert_ids.T
     slots = jnp.transpose(plan_slots, (2, 1, 0))
     lengths = plan_len.T
@@ -431,6 +521,10 @@
     down_tiles = width // (2 * TILE)
     owners = 2 * ranks
     bits = ranks.bit_length() - 1
+    slim = 2 + down_tiles % 2
+    wide = (down_tiles - slim) // 2
+    lanes = kv_blocks.shape[3]
+    request = (states.shape[2] // lanes + per_request * kv_blocks.shape[1], *kv_blocks.shape[2:])
     outputs = pl.pallas_call(
         functools.partial(expert_kernel, ranks, quads),
         out_shape=(
@@ -447,25 +541,28 @@
             pltpu.SMEM(blocks.shape, jnp.int32),
             pltpu.VMEM(tokens.shape, bf16),
             pltpu.VMEM(routes.shape, jnp.float32),
-            pltpu.VMEM((experts, CAP, width), bf16),
+            pltpu.VMEM((PARTS, experts, CAP, width // PARTS), bf16),
             pltpu.VMEM(states.shape, bf16),
             pltpu.VMEM(kv_blocks.shape, bf16),
-            pltpu.VMEM((bits + 1, moves, *state_one), bf16),
-            pltpu.VMEM((bits + 1, moves, per_request, *cache_one), bf16),
-            pltpu.VMEM((bits, moves, *state_one), bf16),
-            pltpu.VMEM((bits, moves, per_request, *cache_one), bf16),
+            pltpu.VMEM((bits + 1, moves, *request), bf16),
+            pltpu.VMEM((bits, moves, *request), bf16),
             pltpu.VMEM((RING, 2, width, TILE), bf16),
-            pltpu.VMEM((quads, ranks, CAP, width), bf16),
+            pltpu.VMEM((PARTS, quads, ranks, CAP, width // PARTS), bf16),
             pltpu.VMEM((quads * ranks * CAP, width), bf16),
+            pltpu.VMEM((SPLIT * WIDE, 2, quads * ranks * CAP, TILE), jnp.float32),
             pltpu.VMEM((quads * ranks * CAP, depth), bf16),
-            pltpu.VMEM((down_tiles, owners * CAP, 2 * TILE), jnp.float32),
-            pltpu.VMEM((down_tiles, owners * CAP, 2 * TILE), jnp.float32),
-            pltpu.VMEM((down_tiles, owners * CAP, 2 * TILE), jnp.float32),
-            pltpu.VMEM((down_tiles, owners, CAP, 2 * TILE), bf16),
-            pltpu.VMEM((down_tiles, owners, CAP, 2 * TILE), bf16),
-            dma((6,)), dma((2,)), dma((RING, 2)), dma, dma((ranks,)), dma, dma((ranks,)), dma((2,)),
-            dma((down_tiles,)), dma((down_tiles,)), dma((down_tiles,)), dma((down_tiles,)),
-            dma((2, bits, moves)), dma((2, bits, moves)),
+            *[
+                spec
+                for count, columns in ((wide, 4 * TILE), (slim, 2 * TILE))
+                for spec in (
+                    pltpu.VMEM((count, owners * CAP, columns), jnp.float32),
+                    pltpu.VMEM((2, count, owners * CAP, columns), jnp.float32),
+                    pltpu.VMEM((2, count, owners, CAP, columns), bf16),
+                )
+            ],
+            dma((6,)), dma((2,)), dma((RING,)), dma, dma((PARTS, ranks)), dma, dma((PARTS, ranks)),
+            dma, dma((PARTS,)),
+            dma, dma((wide + slim,)), dma, dma((wide + slim,)), dma, dma((bits,)),
         ],
         compiler_params=pltpu.CompilerParams(
             collective_id=0, has_side_effects=True, vmem_limit_bytes=VMEM_LIMIT

time: 46.6 us -> 38.2 us (0.82)
  Pallas kernels: 45.8 us -> 37.4 us
    pallas_call x1, Pallas kernels: 44.6 us -> 36.2 us  [fused(): pl.pallas_call(functools.partial(expert_kernel, ranks, quads), out_shape=...]
where the time goes in v2:
time: 38.2 us; the launch traced here: 38 us
  Pallas kernels  37.4 us (98%)
  between operations  0.64 us (2%)
    pallas_call x1, Pallas kernels, fused(): pl.pallas_call(functools.partial(expert_kernel, ranks, quads), out_shape=...  36.2 us
    pallas_call x1, Pallas kernels, fused(): pl.pallas_call(land_kernel, out_shape=(like(states.shape, bf16), like(kv_...  1.17 us

profile of v2, /device:TPU:0, one launch (start us, length us, event | category | flops | bytes accessed | tf_op | source)
XLA Modules:
  0.0 38.0 jit_solution(14875904326477048807)
XLA Ops:
  0.6 36.2 %expert.1 = (bf16[16,16,2048]{2,1,0:T(8,128)(2,1)S(1)}, bf16[32,2,16,256]{3,2,1,0:T(8,128)(2,1)S(1)}, bf16[4,4096]{1,0:T(4,128)(2,1)S(1)}) custom-call(s32[2,4]{1,0:T(2,128)} %bitcast.8, s32[3,2,8]{2,1,0:T(2,128)} %bitcast.7, s32[2,8]{1,0:T(2,128)} %bitcast.9, s32[2,2,2,8]{3,2,1,0:T(2,128)} %bitcast.6, bf16[4,4096]{1,0:T(4,128)(2,1)} %tok_hbm.1, ...), custom_call_target="tpu_custom_call" | custom-call | tf_op jit(solution)/shard_map/expert/pallas_call | solution.py:528
  36.8 1.2 %land.1 = (bf16[16,16,2048]{2,1,0:T(8,128)(2,1)}, bf16[32,2,16,256]{3,2,1,0:T(8,128)(2,1)}, bf16[4,4096]{1,0:T(4,128)(2,1)}) custom-call(bf16[16,16,2048]{2,1,0:T(8,128)(2,1)S(1)} %get-tuple-element.9.states_ref, bf16[32,2,16,256]{3,2,1,0:T(8,128)(2,1)S(1)} %get-tuple-element.10.cache_ref, bf16[4,4096]{1,0:T(4,128)(2,1)S(1)} %get-tuple-element.11.mixed_ref), custom_call_target="tpu_custom_call" | custom-call | tf_op jit(solution)/shard_map/land/pallas_call | solution.py:575

commit v3 on v2

--- a/solution.py
+++ b/solution.py
@@ -16,9 +16,9 @@
 TILE = 256
 RING = 13
 EARLY = 2
-WIDE = 2
+WIDE = 3
 PARTS = 2
-SPLIT = 3
+SPLIT = 6
 LAND_LIMIT = 1 << 20
 
 
@@ -70,15 +70,21 @@
 
     barrier = pltpu.get_barrier_semaphore()
 
-    @pl.loop(1, owners)
-    def _(k):
-        other = lax.rem(me + k, owners)
-        pl.semaphore_signal(
-            barrier, inc=1, device_id=(lax.rem(other, ranks), (other // ranks) * 2 + core),
-            device_id_type=MESH,
-        )
-
-    for quad in (twin, diagonal):
+    z_count = ranks // 2
+
+    def planes(i, reverse):
+        forward = (d // 2 < z_count // 2) == (not reverse)
+        return jnp.where(forward, i, z_count - 1 - i)
+
+    for i in range(z_count):
+        for flip in range(2):
+            other = planes(i, True) * 2 + lax.rem(d + 1 + flip, 2)
+
+            @pl.when(other != d)
+            def _():
+                pl.semaphore_signal(barrier, inc=1, device_id=(other, e), device_id_type=MESH)
+
+    for quad in (across, diagonal, twin):
         pl.semaphore_signal(barrier, inc=1, device_id=(d, quad), device_id_type=MESH)
 
     smalls = [
@@ -154,13 +160,7 @@
             packed_ref[h, r] = packed[r * CAP : (r + 1) * CAP, h * span : (h + 1) * span]
         x_in[h, e, d] = packed_ref[h, d]
 
-    pl.semaphore_wait(barrier, owners + 1)
-
-    z_count = ranks // 2
-
-    def planes(i, reverse):
-        forward = (d // 2 < z_count // 2) == (not reverse)
-        return jnp.where(forward, i, z_count - 1 - i)
+    pl.semaphore_wait(barrier, ranks + 2)
 
     def cross(src, h, source):
         return pltpu.make_async_remote_copy(
@@ -323,64 +323,60 @@
 
     def finish_up(j, gate, upper):
         value = gate / (1.0 + jnp.exp(-gate)) * upper
-        hidden[:, pl.ds(pl.multiple_of(j * TILE, TILE), TILE)] = value.astype(jnp.bfloat16)
+        hidden[:, j * TILE : (j + 1) * TILE] = value.astype(jnp.bfloat16)
 
     def refill(j):
         later = j + ring - up_tiles
 
-        @pl.when(later < down_tiles)
-        def _():
+        if later < down_tiles:
             for copy in down_copies(later):
                 copy.start()
 
-    def tiles_of(i):
-        return [i * WIDE + n for n in range(WIDE)]
-
-    def first_step(i):
-        for j in tiles_of(i):
+    def first_step(tiles):
+        for j in tiles:
             up_wait(j)
-        for j in tiles_of(i):
+        for j in tiles:
             for which in range(2):
                 part_sum[j, which] = product(j, which, 0)
 
-    def second_step(i):
-        for j in tiles_of(i):
+    def second_step(tiles):
+        for j in tiles:
             sums = [part_sum[j, which] for which in range(2)]
             for h in range(1, PARTS):
                 sums = [sums[which] + product(j, which, h) for which in range(2)]
             finish_up(j, *sums)
-        for j in tiles_of(i):
+        for j in tiles:
             refill(j)
 
-    def whole_step(i):
-        for j in tiles_of(i):
+    def whole_step(tiles):
+        for j in tiles:
             up_wait(j)
-        for j in tiles_of(i):
+        for j in tiles:
             gate, upper = [
                 jnp.dot(x_all[...], w_buf[j, which], preferred_element_type=jnp.float32)
                 for which in range(2)
             ]
             finish_up(j, gate, upper)
-        for j in tiles_of(i):
+        for j in tiles:
             refill(j)
 
-    split = part_sum.shape[0] // WIDE
-    pl.loop(0, split - 1)(first_step)
+    split = part_sum.shape[0]
+    early = split - 2
+    first_step(range(early))
     for h in range(1, PARTS):
         relay(h)
         gather(h, core)
-    pl.loop(split - 1, split)(first_step)
+    first_step(range(early, split))
     for h in range(1, PARTS):
         pair_wait(h)
         gather(h, 1 - core)
-    hop_finish(0)
-    hop_start(1)
-    pl.loop(0, split)(second_step)
-    pl.loop(split, up_tiles // WIDE)(whole_step)
-    for step in range(1, bits - 1):
-        hop_finish(step)
-        hop_start(step + 1)
-
+    for start in range(0, split, WIDE):
+        second_step(range(start, min(start + WIDE, split)))
+        if start == 0:
+            hop_finish(0)
+            hop_start(1)
+    for start in range(split, up_tiles, WIDE):
+        whole_step(range(start, min(start + WIDE, up_tiles)))
     wide_count = wide_keep.shape[0]
     groups = [(0, g, 2 * g, 2) for g in range(wide_count)]
     groups += [(1, g, 2 * wide_count + g, 1) for g in range(slim_keep.shape[0])]
@@ -443,9 +439,13 @@
         multiply(n)
         if n > 0:
             send_home(n - 1)
+        else:
+            for step in range(1, bits - 1):
+                hop_finish(step)
+                hop_start(step + 1)
     send_home(len(groups) - 1)
-    early = max(len(groups) - 2, 0)
-    for n in range(early):
+    mixed_early = max(len(groups) - 2, 0)
+    for n in range(mixed_early):
         mix(n)
     hop_finish(bits - 1)
 
@@ -483,7 +483,7 @@
                 value = lax.select(landing[m][1][j] == s, pay[bits, m, pl.ds(pieces + 2 * j, 2)], value)
         new_cache[s] = value
 
-    for n in range(early, len(groups)):
+    for n in range(mixed_early, len(groups)):
         mix(n)
 
     for step in range(bits):
@@ -549,7 +549,7 @@
             pltpu.VMEM((RING, 2, width, TILE), bf16),
             pltpu.VMEM((PARTS, quads, ranks, CAP, width // PARTS), bf16),
             pltpu.VMEM((quads * ranks * CAP, width), bf16),
-            pltpu.VMEM((SPLIT * WIDE, 2, quads * ranks * CAP, TILE), jnp.float32),
+            pltpu.VMEM((SPLIT, 2, quads * ranks * CAP, TILE), jnp.float32),
             pltpu.VMEM((quads * ranks * CAP, depth), bf16),
             *[
                 spec

time: 38.2 us -> 37.5 us (0.982)
  Pallas kernels: 37.4 us -> 36.7 us
    pallas_call x1, Pallas kernels: 36.2 us -> 35.5 us  [fused(): pl.pallas_call(functools.partial(expert_kernel, ranks, quads), out_shape=...]
where the time goes in v3:
time: 37.5 us; the launch traced here: 37.3 us
  Pallas kernels  36.7 us (98%)
  between operations  0.64 us (2%)
    pallas_call x1, Pallas kernels, fused(): pl.pallas_call(functools.partial(expert_kernel, ranks, quads), out_shape=...  35.5 us
    pallas_call x1, Pallas kernels, fused(): pl.pallas_call(land_kernel, out_shape=(like(states.shape, bf16), like(kv_...  1.17 us

profile of v3, /device:TPU:0, one launch (start us, length us, event | category | flops | bytes accessed | tf_op | source)
XLA Modules:
  0.0 37.3 jit_solution(17882878087636318491)
XLA Ops:
  0.6 35.5 %expert.1 = (bf16[16,16,2048]{2,1,0:T(8,128)(2,1)S(1)}, bf16[32,2,16,256]{3,2,1,0:T(8,128)(2,1)S(1)}, bf16[4,4096]{1,0:T(4,128)(2,1)S(1)}) custom-call(s32[2,4]{1,0:T(2,128)} %bitcast.8, s32[3,2,8]{2,1,0:T(2,128)} %bitcast.7, s32[2,8]{1,0:T(2,128)} %bitcast.9, s32[2,2,2,8]{3,2,1,0:T(2,128)} %bitcast.6, bf16[4,4096]{1,0:T(4,128)(2,1)} %tok_hbm.1, ...), custom_call_target="tpu_custom_call" | custom-call | tf_op jit(solution)/shard_map/expert/pallas_call | solution.py:528
  36.2 1.2 %land.1 = (bf16[16,16,2048]{2,1,0:T(8,128)(2,1)}, bf16[32,2,16,256]{3,2,1,0:T(8,128)(2,1)}, bf16[4,4096]{1,0:T(4,128)(2,1)}) custom-call(bf16[16,16,2048]{2,1,0:T(8,128)(2,1)S(1)} %get-tuple-element.9.states_ref, bf16[32,2,16,256]{3,2,1,0:T(8,128)(2,1)S(1)} %get-tuple-element.10.cache_ref, bf16[4,4096]{1,0:T(4,128)(2,1)S(1)} %get-tuple-element.11.mixed_ref), custom_call_target="tpu_custom_call" | custom-call | tf_op jit(solution)/shard_map/land/pallas_call | solution.py:575

commit v4 on v3

--- a/solution.py
+++ b/solution.py
@@ -162,25 +162,20 @@
 
     pl.semaphore_wait(barrier, ranks + 2)
 
-    def cross(src, h, source):
+    def pair_of(h, quad, plane):
+        return x_in.at[h, quad, pl.ds(plane * 2, 2)]
+
+    def cross(h, quad, plane):
         return pltpu.make_async_remote_copy(
-            src, x_in.at[h, e, source], cross_send, cross_recv.at[h, source],
+            pair_of(h, quad, plane), pair_of(h, e, plane), cross_send, cross_recv.at[h, plane],
             device_id=(d, across), device_id_type=MESH,
         )
 
-    def to_other(src, h, quad, source, where):
+    def to_other(h, quad, plane, where):
         return pltpu.make_async_remote_copy(
-            src, x_in.at[h, quad, source], pair_send, pair_recv.at[h],
+            pair_of(h, quad, plane), pair_of(h, quad, plane), pair_send, pair_recv.at[h],
             device_id=(d, where), device_id_type=MESH,
         )
-
-    def spread(src, h, source):
-        cross(src, h, source).start()
-        to_other(src, h, e, source, twin).start()
-
-        @pl.when(core == 0)
-        def _():
-            to_other(src, h, e, source, diagonal).start()
 
     for h in range(PARTS):
         for i in range(z_count):
@@ -191,11 +186,10 @@
                 @pl.when(peer != d)
                 def _():
                     pltpu.make_async_remote_copy(
-                        packed_ref.at[h, peer], x_in.at[h, e, d], first_send, first_recv.at[h, d],
+                        packed_ref.at[h, peer], x_in.at[h, e, d], first_send, first_recv.at[h, d // 2],
                         device_id=(peer, e), device_id_type=MESH,
                     ).start()
 
-        spread(packed_ref.at[h, d], h, d)
 
     smalls[2].wait()
     wide = tok_ref[...].astype(jnp.float32)
@@ -223,26 +217,31 @@
     comb_high = comb.astype(jnp.bfloat16)
     comb_low = (comb - comb_high.astype(jnp.float32)).astype(jnp.bfloat16)
 
-    near = [planes(i, False) * 2 + y for i in range(z_count) for y in range(2)]
+    near = [planes(i, False) for i in range(z_count)]
 
     def relay(h):
-        for source in near:
-            cross(x_in.at[h, across, source], h, source).wait_recv()
+        for plane in near:
+            cross(h, across, plane).wait_recv()
 
             @pl.when(core == 1)
             def _():
-                to_other(x_in.at[h, across, source], h, across, source, twin).start()
+                to_other(h, across, plane, twin).start()
 
     for h in range(PARTS):
-        for source in near:
-
-            @pl.when(source != d)
+        for plane in near:
+            for count in range(1, 3):
+
+                @pl.when((plane == d // 2) == (count == 1))
+                def _():
+                    most = x_in.at[h, e, pl.ds(0, count)]
+                    pltpu.make_async_copy(most, most, first_recv.at[h, plane]).wait()
+
+            cross(h, e, plane).start()
+            to_other(h, e, plane, twin).start()
+
+            @pl.when(core == 0)
             def _():
-                pltpu.make_async_remote_copy(
-                    packed_ref.at[h, d], x_in.at[h, e, source], first_send, first_recv.at[h, source],
-                    device_id=(source, e), device_id_type=MESH,
-                ).wait_recv()
-                spread(x_in.at[h, e, source], h, source)
+                to_other(h, e, plane, diagonal).start()
 
     for copy in smalls[3:]:
         copy.wait()
@@ -444,9 +443,6 @@
                 hop_finish(step)
                 hop_start(step + 1)
     send_home(len(groups) - 1)
-    mixed_early = max(len(groups) - 2, 0)
-    for n in range(mixed_early):
-        mix(n)
     hop_finish(bits - 1)
 
     leaving, landing = [], []
@@ -483,7 +479,7 @@
                 value = lax.select(landing[m][1][j] == s, pay[bits, m, pl.ds(pieces + 2 * j, 2)], value)
         new_cache[s] = value
 
-    for n in range(mixed_early, len(groups)):
+    for n in range(len(groups)):
         mix(n)
 
     for step in range(bits):
@@ -560,7 +556,7 @@
                     pltpu.VMEM((2, count, owners, CAP, columns), bf16),
                 )
             ],
-            dma((6,)), dma((2,)), dma((RING,)), dma, dma((PARTS, ranks)), dma, dma((PARTS, ranks)),
+            dma((6,)), dma((2,)), dma((RING,)), dma, dma((PARTS, ranks // 2)), dma, dma((PARTS, ranks // 2)),
             dma, dma((PARTS,)),
             dma, dma((wide + slim,)), dma, dma((wide + slim,)), dma, dma((bits,)),
         ],

time: 37.5 us -> 37.3 us (level)
  no operation moved by 1% of the time
where the time goes in v4:
time: 37.3 us; the launch traced here: 37.2 us
  Pallas kernels  36.5 us (98%)
  between operations  0.64 us (2%)
    pallas_call x1, Pallas kernels, fused(): pl.pallas_call(functools.partial(expert_kernel, ranks, quads), out_shape=...  35.4 us
    pallas_call x1, Pallas kernels, fused(): pl.pallas_call(land_kernel, out_shape=(like(states.shape, bf16), like(kv_...  1.17 us

profile of v4, /device:TPU:0, one launch (start us, length us, event | category | flops | bytes accessed | tf_op | source)
XLA Modules:
  0.0 37.2 jit_solution(9613038997989189124)
XLA Ops:
  0.6 35.4 %expert.1 = (bf16[16,16,2048]{2,1,0:T(8,128)(2,1)S(1)}, bf16[32,2,16,256]{3,2,1,0:T(8,128)(2,1)S(1)}, bf16[4,4096]{1,0:T(4,128)(2,1)S(1)}) custom-call(s32[2,4]{1,0:T(2,128)} %bitcast.8, s32[3,2,8]{2,1,0:T(2,128)} %bitcast.7, s32[2,8]{1,0:T(2,128)} %bitcast.9, s32[2,2,2,8]{3,2,1,0:T(2,128)} %bitcast.6, bf16[4,4096]{1,0:T(4,128)(2,1)} %tok_hbm.1, ...), custom_call_target="tpu_custom_call" | custom-call | tf_op jit(solution)/shard_map/expert/pallas_call | solution.py:524
  36.0 1.2 %land.1 = (bf16[16,16,2048]{2,1,0:T(8,128)(2,1)}, bf16[32,2,16,256]{3,2,1,0:T(8,128)(2,1)}, bf16[4,4096]{1,0:T(4,128)(2,1)}) custom-call(bf16[16,16,2048]{2,1,0:T(8,128)(2,1)S(1)} %get-tuple-element.9.states_ref, bf16[32,2,16,256]{3,2,1,0:T(8,128)(2,1)S(1)} %get-tuple-element.10.cache_ref, bf16[4,4096]{1,0:T(4,128)(2,1)S(1)} %get-tuple-element.11.mixed_ref), custom_call_target="tpu_custom_call" | custom-call | tf_op jit(solution)/shard_map/land/pallas_call | solution.py:571

commit v5 on v4

--- a/solution.py
+++ b/solution.py
@@ -393,7 +393,7 @@
         kind, g, _, _ = groups[n]
         keep, pair, home = stores[kind]
         swap_copy(n).wait_recv()
-        whole = (keep[g] + pair[1, g]).astype(jnp.bfloat16)
+        whole = (keep[g] + pair[1, g].astype(jnp.float32)).astype(jnp.bfloat16)
         for o in range(owners):
             home[0, g, o] = whole[o * CAP : (o + 1) * CAP]
         home[1, g, me] = home[0, g, me]
@@ -421,7 +421,7 @@
                 first = core == 0
                 columns = pl.ds((2 * (c - start) + h) * TILE, TILE)
                 keep[g, :, columns] = lax.select(first, low, high)
-                pair[0, g, :, columns] = lax.select(first, high, low)
+                pair[0, g, :, columns] = lax.select(first, high, low).astype(jnp.bfloat16)
         swap_copy(n).start()
 
     def mix(n):
@@ -552,7 +552,7 @@
                 for count, columns in ((wide, 4 * TILE), (slim, 2 * TILE))
                 for spec in (
                     pltpu.VMEM((count, owners * CAP, columns), jnp.float32),
-                    pltpu.VMEM((2, count, owners * CAP, columns), jnp.float32),
+                    pltpu.VMEM((2, count, owners * CAP, columns), bf16),
                     pltpu.VMEM((2, count, owners, CAP, columns), bf16),
                 )
             ],

time: 37.3 us -> 37.2 us (level)
  no operation moved by 1% of the time
where the time goes in v5:
time: 37.2 us; the launch traced here: 37.1 us
  Pallas kernels  36.4 us (98%)
  between operations  0.64 us (2%)
    pallas_call x1, Pallas kernels, fused(): pl.pallas_call(functools.partial(expert_kernel, ranks, quads), out_shape=...  35.2 us
    pallas_call x1, Pallas kernels, fused(): pl.pallas_call(land_kernel, out_shape=(like(states.shape, bf16), like(kv_...  1.17 us

profile of v5, /device:TPU:0, one launch (start us, length us, event | category | flops | bytes accessed | tf_op | source)
XLA Modules:
  0.0 37.1 jit_solution(18333074062790143326)
XLA Ops:
  0.6 35.2 %expert.1 = (bf16[16,16,2048]{2,1,0:T(8,128)(2,1)S(1)}, bf16[32,2,16,256]{3,2,1,0:T(8,128)(2,1)S(1)}, bf16[4,4096]{1,0:T(4,128)(2,1)S(1)}) custom-call(s32[2,4]{1,0:T(2,128)} %bitcast.8, s32[3,2,8]{2,1,0:T(2,128)} %bitcast.7, s32[2,8]{1,0:T(2,128)} %bitcast.9, s32[2,2,2,8]{3,2,1,0:T(2,128)} %bitcast.6, bf16[4,4096]{1,0:T(4,128)(2,1)} %tok_hbm.1, ...), custom_call_target="tpu_custom_call" | custom-call | tf_op jit(solution)/shard_map/expert/pallas_call | solution.py:524
  35.9 1.2 %land.1 = (bf16[16,16,2048]{2,1,0:T(8,128)(2,1)}, bf16[32,2,16,256]{3,2,1,0:T(8,128)(2,1)}, bf16[4,4096]{1,0:T(4,128)(2,1)}) custom-call(bf16[16,16,2048]{2,1,0:T(8,128)(2,1)S(1)} %get-tuple-element.9.states_ref, bf16[32,2,16,256]{3,2,1,0:T(8,128)(2,1)S(1)} %get-tuple-element.10.cache_ref, bf16[4,4096]{1,0:T(4,128)(2,1)S(1)} %get-tuple-element.11.mixed_ref), custom_call_target="tpu_custom_call" | custom-call | tf_op jit(solution)/shard_map/land/pallas_call | solution.py:571
